TPU v7x, 512 devices: a whole 4x8x8 slice. The times are simulated.
512 devices in a mesh: mem: 64 (over z, x, core), gy: 8 (over y).
Axes of the slice: x: 4, y: 8, z: 8, core: 2. Of those that a mesh axis runs over, the one named last changes fastest.
Arguments:
- state: bfloat16 [64, 2, 2048, 1024], P('mem', None, None, 'gy'), may hold values from -6 to 6
- obs_index: int32 [64, 8, 256], P('mem', 'gy'), may hold values from 0 to 8191
- obs_count: int32 [64, 8], P('mem', 'gy'), may hold values from 1 to 256, as said below
- obs_value: float32 [64, 8, 256], P('mem', 'gy'), may hold values from -6 to 6
- obs_var: float32 [64, 8, 256], P('mem', 'gy'), may hold values from 0.1 to 1
- radius: int32 [64, 8], P('mem', 'gy'), may hold values from 8 to 16
Outputs:
- analysis: bfloat16 [64, 2, 2048, 1024], P('mem', None, None, 'gy')
Inputs may be any that keep to these rules, and one draw needn't show every extreme that they name: `obs_count`: Tiles' counts are skewed: most tiles have few live slots, some many, and in every draw some tile has all 256 slots live.
All inputs are finite; a program needn't handle non-finite values.
Results may differ from a plain program's by a relative error of at most 0.0028.
The roundings to bfloat16 on the way count: a program that leaves them out, or rounds other values in their place, can miss the bound.
Values may be sent and summed in bfloat16 or wider, within the bound.
A program may use at most 64 MiB of HBM per device.

v0:
```python
import jax
import jax.numpy as jnp
from jax import lax
from jax.sharding import PartitionSpec as P

K = 64
LEV = 2
ROWS = 128
COLS = 32
BLK = 16
NSI = 10


highest = lax.Precision.HIGHEST


def extended(cells, sides, width):
    for axis, dim in sides:
        count = lax.axis_size(axis)
        ends = count - 1
        head = lax.slice_in_dim(cells, 0, width, axis=dim)
        tail = lax.slice_in_dim(cells, cells.shape[dim] - width, cells.shape[dim], axis=dim)
        cells = jnp.concatenate(
            [
                lax.ppermute(tail, axis, [(i, (i + 1) % count) for i in range(ends)]),
                cells,
                lax.ppermute(head, axis, [((i + 1) % count, i) for i in range(ends)]),
            ],
            axis=dim,
        )
    return cells


def build_payload(ensemble, obs_slots, live_count, observed, variance):
    slot_total = obs_slots.shape[0]
    centre = jnp.mean(ensemble, axis=0)
    spread = ensemble - centre
    is_live = jnp.arange(slot_total, dtype=jnp.int32) < live_count
    weight = jnp.where(is_live, 1.0 / variance, jnp.zeros_like(variance))
    innovation = observed - centre
    col_pos = (obs_slots // ROWS % COLS).astype(jnp.float32)
    row_pos = (obs_slots % ROWS).astype(jnp.float32)
    return jnp.concatenate(
        [spread, innovation[None], weight[None], col_pos[None], row_pos[None]], axis=0
    )


def transforms(payload, radius):
    nearby = extended(payload[None, None], (("mem", 0), ("gy", 1)), 1)
    count_c = COLS // BLK
    count_r = ROWS // BLK
    block_ids = jnp.arange(count_c * count_r, dtype=jnp.int32)
    centre_c = (block_ids // count_r * BLK).astype(jnp.float32) + (BLK - 1) / 2.0
    centre_r = (block_ids % count_r * BLK).astype(jnp.float32) + (BLK - 1) / 2.0
    reach_sq = jnp.square(radius[0].astype(jnp.float32))
    gram_sum = jnp.zeros((count_c * count_r, K, K), jnp.float32)
    drive_sum = jnp.zeros((count_c * count_r, K), jnp.float32)
    for step_x in range(3):
        for step_y in range(3):
            neighbour = nearby[step_x, step_y]
            spread = neighbour[:K]
            innovation = neighbour[K]
            weight = neighbour[K + 1]
            gap_c = (step_x - 1) * COLS + neighbour[K + 2][None, :] - centre_c[:, None]
            gap_r = (step_y - 1) * ROWS + neighbour[K + 3][None, :] - centre_r[:, None]
            taper_val = jnp.square(
                jnp.maximum(1.0 - (gap_c * gap_c + gap_r * gap_r) / reach_sq, 0.0)
            )
            local_weight = taper_val * weight[None, :]
            weighted = local_weight[:, None, :] * spread[None]
            gram_sum = gram_sum + jnp.einsum("bko,jo->bkj", weighted, spread, precision=highest)
            drive_sum = drive_sum + jnp.einsum("bko,o->bk", weighted, innovation, precision=highest)
    identity = jnp.eye(K, dtype=jnp.float32)
    system = (K - 1.0) * identity + gram_sum
    trace_scale = jnp.trace(system, axis1=1, axis2=2)

    def newton_step(sweep, carry):
        upper_iter, lower_iter = carry
        factor = 1.5 * identity - 0.5 * jnp.einsum(
            "bij,bjk->bik", lower_iter, upper_iter, precision=highest
        )
        return (
            jnp.einsum("bij,bjk->bik", upper_iter, factor, precision=highest),
            jnp.einsum("bij,bjk->bik", factor, lower_iter, precision=highest),
        )

    start = (system / trace_scale[:, None, None], jnp.broadcast_to(identity, system.shape))
    upper_iter, lower_iter = lax.fori_loop(0, NSI, newton_step, start)
    inv_root = lower_iter / jnp.sqrt(trace_scale)[:, None, None]
    posterior = jnp.einsum("bij,bjk->bik", inv_root, inv_root, precision=highest)
    mean_shift = jnp.einsum("bkj,bj->bk", posterior, drive_sum, precision=highest)
    transform = jnp.sqrt(K - 1.0) * inv_root + mean_shift[:, :, None]
    mixing = 1.0 / K + transform - jnp.mean(transform, axis=1, keepdims=True)
    return mixing.astype(jnp.bfloat16)


def mix_tile(tile_state, mixing):
    count_c = COLS // BLK
    count_r = ROWS // BLK
    blocks = tile_state.reshape(K, LEV, count_c, BLK, count_r, BLK)
    mix_table = mixing.reshape(count_c, count_r, K, K)
    mixed_tile = jnp.einsum(
        "abkm,klaibj->mlaibj", mix_table, blocks, preferred_element_type=jnp.float32
    )
    return mixed_tile.reshape(K, LEV, COLS, ROWS).astype(jnp.bfloat16)


def local(state, obs_index, obs_count, obs_value, obs_var, radius):
    obs_slots = obs_index[0, 0]
    live_count = obs_count[0, 0]
    observed = obs_value[0, 0]
    variance = obs_var[0, 0]
    tile_radius = radius[0, 0][None]
    tile_state = lax.all_to_all(state, "mem", split_axis=2, concat_axis=0, tiled=True)
    ensemble = jnp.take(tile_state.reshape(K, LEV * COLS * ROWS), obs_slots, axis=1).astype(
        jnp.float32
    )
    mixing = transforms(
        build_payload(ensemble, obs_slots, live_count, observed, variance), tile_radius
    )
    analysed = mix_tile(tile_state, mixing)
    return lax.all_to_all(analysed, "mem", split_axis=0, concat_axis=2, tiled=True)


def solution(mesh):
    in_specs = (
        P("mem", None, None, "gy"),
        P("mem", "gy", None),
        P("mem", "gy"),
        P("mem", "gy", None),
        P("mem", "gy", None),
        P("mem", "gy"),
    )
    out_specs = P("mem", None, None, "gy")
    return jax.shard_map(local, mesh=mesh, in_specs=in_specs, out_specs=out_specs, check_vma=False)
```

profile of v0, /device:TPU:1, one launch (start us, length us, event | category | flops | bytes accessed | tf_op | source)
XLA Modules:
  0.0 164.0 jit_solution(17580957605853535164)
XLA Ops:
  0.0 3.6 %copy.33 = bf16[1,2,2048,128]{3,1,0,2:T(2,128)(2,1)} copy(bf16[1,2,2048,128]{3,2,1,0:T(8,128)(2,1)} %param.8) | data formatting | bytes 2097152 | tf_op args[0]
  3.6 14.8 %all-to-all-start = ((bf16[1,2,2048,128]{3,1,0,2:T(2,128)(2,1)}), bf16[1,2,2048,128]{3,1,0,2:T(2,128)(2,1)S(1)}, u32[]{:S(2)}, u32[]{:S(2)}) async-start(bf16[1,2,2048,128]{3,1,0,2:T(2,128)(2,1)} %copy.33), calls=%async_computation | async-start | bytes 2097152 | tf_op jit(solution)/shard_map/all_to_all | solution.py:114
  19.9 26.7 %all-to-all-done = bf16[1,2,2048,128]{3,1,0,2:T(2,128)(2,1)S(1)} async-done(((bf16[1,2,2048,128]{3,1,0,2:T(2,128)(2,1)}), bf16[1,2,2048,128]{3,1,0,2:T(2,128)(2,1)S(1)}, u32[]{:S(2)}, u32[]{:S(2)}) %all-to-all-start) | async-done | bytes 1048608 | tf_op jit(solution)/shard_map/all_to_all | solution.py:114
  46.8 1.5 copy.35
  49.3 4.1 %collective-permute-start = (f32[1,1,68,256]{3,2,1,0:T(8,128)S(1)}, f32[1,1,68,256]{3,2,1,0:T(8,128)S(1)}, u32[]{:S(2)}, u32[]{:S(2)}) collective-permute-start(f32[1,1,68,256]{3,2,1,0:T(8,128)S(1)} %bitcast.222), channel_id=1, source_target_pairs={{0,8},{8,16},{16,24},{24,32},{32,40},{40,48},{48,56},{56,64},{64,7... | collective-permute-start | bytes 208904 | tf_op jit(solution)/shard_map/ppermute | solution.py:25
  53.5 1.9 %collective-permute-start.1 = (f32[1,1,68,256]{3,2,1,0:T(8,128)S(1)}, f32[1,1,68,256]{3,2,1,0:T(8,128)S(1)}, u32[]{:S(2)}, u32[]{:S(2)}) collective-permute-start(f32[1,1,68,256]{3,2,1,0:T(8,128)S(1)} %bitcast.223), channel_id=1, source_target_pairs={{8,0},{16,8},{24,16},{32,24},{40,32},{48,40},{56,48},{64,56},{72,6... | collective-permute-start | bytes 208904 | tf_op jit(solution)/shard_map/ppermute | solution.py:27
  55.4 3.7 %collective-permute-done.1 = f32[1,1,68,256]{3,2,1,0:T(8,128)S(1)} collective-permute-done((f32[1,1,68,256]{3,2,1,0:T(8,128)S(1)}, f32[1,1,68,256]{3,2,1,0:T(8,128)S(1)}, u32[]{:S(2)}, u32[]{:S(2)}) %collective-permute-start.1) | collective-permute-done | bytes 69664 | tf_op jit(solution)/shard_map/ppermute | solution.py:27
  59.2 1.3 collective-permute-start.3
  60.5 4.2 %collective-permute-start.2 = (f32[3,1,68,256]{3,2,1,0:T(8,128)S(1)}, f32[3,1,68,256]{3,2,1,0:T(8,128)S(1)}, u32[]{:S(2)}, u32[]{:S(2)}) collective-permute-start(f32[3,1,68,256]{3,2,1,0:T(8,128)S(1)} %pad_maximum_fusion), channel_id=1, source_target_pairs={{0,1},{1,2},{2,3},{3,4},{4,5},{5,6},{6,7},{8,9},{9,10},{10,11},{11... | collective-permute-start | bytes 626696 | tf_op jit(solution)/shard_map/ppermute | solution.py:25
  64.7 1.4 collective-permute-done.3
  66.2 1.7 %collective-permute-done.2 = f32[3,1,68,256]{3,2,1,0:T(8,128)S(1)} collective-permute-done((f32[3,1,68,256]{3,2,1,0:T(8,128)S(1)}, f32[3,1,68,256]{3,2,1,0:T(8,128)S(1)}, u32[]{:S(2)}, u32[]{:S(2)}) %collective-permute-start.2) | collective-permute-done | bytes 208928 | tf_op jit(solution)/shard_map/ppermute | solution.py:25
  69.1 1.4 fusion.24
  77.8 1.1 select_reduce_fusion
  79.8 27.7 %while.13 = (s32[]{:T(128)}, f32[16,64,64]{1,2,0:T(8,128)S(1)}, f32[16,64,64]{2,1,0:T(8,128)S(1)}, s32[]{:T(128)}) while((s32[]{:T(128)}, f32[16,64,64]{1,2,0:T(8,128)S(1)}, f32[16,64,64]{2,1,0:T(8,128)S(1)}, s32[]{:T(128)}) %tuple.63), condition=%wide.region_3.4_spmd.clone, body=%wide.region_2.3_spmd.clone.sunk | while | flops 151134208 | bytes 3440693 | solution.py:88
  81.5 1.0 convolution_bitcast_fusion.2
  87.0 1.0 convolution_bitcast_fusion.2
  89.8 1.0 convolution_bitcast_fusion.2
  92.5 1.0 convolution_bitcast_fusion.2
  98.0 1.0 convolution_bitcast_fusion.2
  100.8 1.0 convolution_bitcast_fusion.2
  103.5 1.0 convolution_bitcast_fusion.2
  108.4 2.2 %fusion.36 = f32[1,16,64]{2,0,1:T(1,128)S(1)} fusion(f32[64,256]{1,0:T(8,128)} %copy-done.7, f32[16,256]{1,0:T(8,128)S(1)} %copy-done.31, f32[1,1,68,256]{3,2,1,0:T(8,128)S(1)} %collective-permute-done), kind=kOutput, calls=%fused_computation.38 | convolution fusion | flops 3407872 | bytes 87040 | tf_op jit(solution)/shard_map/bko,o->bk/dot_general | solution.py:72
  110.7 2.1 %fusion.40 = f32[1,16,64]{2,0,1:T(1,128)S(1)} fusion(f32[64,256]{1,0:T(8,128)S(1)} %copy-done.4, f32[16,256]{1,0:T(8,128)S(1)} %copy-done.17, f32[3,1,68,256]{3,2,1,0:T(8,128)} %copy-done), kind=kOutput, calls=%fused_computation.42 | convolution fusion | flops 3407872 | bytes 87040 | tf_op jit(solution)/shard_map/bko,o->bk/dot_general | solution.py:72
  112.8 1.4 fusion.32
  114.1 2.1 %fusion.28 = f32[1,16,64]{2,0,1:T(1,128)S(1)} fusion(f32[64,256]{1,0:T(8,128)S(1)} %copy-done.13, f32[16,256]{1,0:T(8,128)S(1)} %copy-done.27, f32[3,1,68,256]{3,2,1,0:T(8,128)} %copy-done), kind=kOutput, calls=%fused_computation.30 | convolution fusion | flops 3407872 | bytes 87040 | tf_op jit(solution)/shard_map/bko,o->bk/dot_general | solution.py:72
  116.2 1.4 fusion.20
  117.6 2.1 %fusion.16 = f32[1,16,64]{2,0,1:T(1,128)S(1)} fusion(f32[64,256]{1,0:T(8,128)S(1)} %copy-done.11, f32[16,256]{1,0:T(8,128)S(1)} %copy-done.25, f32[3,1,68,256]{3,2,1,0:T(8,128)} %copy-done), kind=kOutput, calls=%fused_computation.18 | convolution fusion | flops 3407872 | bytes 87040 | tf_op jit(solution)/shard_map/bko,o->bk/dot_general | solution.py:72
  119.7 1.4 fusion.12
  121.1 1.4 fusion.8
  125.2 1.7 %copy.41 = bf16[64,2,32,128]{3,2,1,0:T(8,128)(2,1)S(1)} copy(bf16[64,2,32,128]{0,3,2,1:T(8,128)(2,1)S(1)} %bitcast.219) | data formatting | bytes 2097152 | tf_op jit(solution)/shard_map/convert_element_type | solution.py:105
  126.9 36.0 %all_to_all.33 = bf16[64,2,32,128]{3,2,1,0:T(8,128)(2,1)S(1)} all-to-all(bf16[64,2,32,128]{3,2,1,0:T(8,128)(2,1)S(1)} %copy.41), channel_id=1, replica_groups=mesh['mem'=64,'gy'=8] {'mem'}, dimensions={0} | all-to-all | bytes 2097152 | tf_op jit(solution)/shard_map/all_to_all | solution.py:122
  162.9 1.1 copy.42
  (178 shorter events, 33.9 us)
Async XLA Ops:
  0.0 19.8 %copy-start.32 = (s32[1,1,256]{2,1,0:T(1,128)S(1)}, s32[1,1,256]{2,1,0:T(1,128)}, u32[]{:S(2)}) copy-start(s32[1,1,256]{2,1,0:T(1,128)} %param.9) | copy-start | bytes 3076
  3.6 43.0 %all-to-all-start = ((bf16[1,2,2048,128]{3,1,0,2:T(2,128)(2,1)}), bf16[1,2,2048,128]{3,1,0,2:T(2,128)(2,1)S(1)}, u32[]{:S(2)}, u32[]{:S(2)}) async-start(bf16[1,2,2048,128]{3,1,0,2:T(2,128)(2,1)} %copy.33), calls=%async_computation | async-start | bytes 2097152 | tf_op jit(solution)/shard_map/all_to_all | solution.py:114
  49.3 6.1 %collective-permute-start = (f32[1,1,68,256]{3,2,1,0:T(8,128)S(1)}, f32[1,1,68,256]{3,2,1,0:T(8,128)S(1)}, u32[]{:S(2)}, u32[]{:S(2)}) collective-permute-start(f32[1,1,68,256]{3,2,1,0:T(8,128)S(1)} %bitcast.222), channel_id=1, source_target_pairs={{0,8},{8,16},{16,24},{24,32},{32,40},{40,48},{48,56},{56,64},{64,7... | collective-permute-start | bytes 208904 | tf_op jit(solution)/shard_map/ppermute | solution.py:25
  53.5 5.7 %collective-permute-start.1 = (f32[1,1,68,256]{3,2,1,0:T(8,128)S(1)}, f32[1,1,68,256]{3,2,1,0:T(8,128)S(1)}, u32[]{:S(2)}, u32[]{:S(2)}) collective-permute-start(f32[1,1,68,256]{3,2,1,0:T(8,128)S(1)} %bitcast.223), channel_id=1, source_target_pairs={{8,0},{16,8},{24,16},{32,24},{40,32},{48,40},{56,48},{64,56},{72,6... | collective-permute-start | bytes 208904 | tf_op jit(solution)/shard_map/ppermute | solution.py:27
  59.2 7.0 %collective-permute-start.3 = (f32[3,1,68,256]{3,2,1,0:T(8,128)S(1)}, f32[3,1,68,256]{3,2,1,0:T(8,128)S(1)}, u32[]{:S(2)}, u32[]{:S(2)}) collective-permute-start(f32[3,1,68,256]{3,2,1,0:T(8,128)S(1)} %pad_maximum_fusion), channel_id=1, source_target_pairs={{1,0},{2,1},{3,2},{4,3},{5,4},{6,5},{7,6},{9,8},{10,9},{11,10},{12... | collective-permute-start | bytes 626696 | tf_op jit(solution)/shard_map/ppermute | solution.py:27
  60.5 7.5 %collective-permute-start.2 = (f32[3,1,68,256]{3,2,1,0:T(8,128)S(1)}, f32[3,1,68,256]{3,2,1,0:T(8,128)S(1)}, u32[]{:S(2)}, u32[]{:S(2)}) collective-permute-start(f32[3,1,68,256]{3,2,1,0:T(8,128)S(1)} %pad_maximum_fusion), channel_id=1, source_target_pairs={{0,1},{1,2},{2,3},{3,4},{4,5},{5,6},{6,7},{8,9},{9,10},{10,11},{11... | collective-permute-start | bytes 626696 | tf_op jit(solution)/shard_map/ppermute | solution.py:25
  64.7 9.0 %copy-start.7 = (f32[64,256]{1,0:T(8,128)}, f32[64,256]{1,0:T(8,128)S(1)}, u32[]{:S(2)}) copy-start(f32[64,256]{1,0:T(8,128)S(1)} %slice_bitcast_fusion.6) | copy-start | bytes 196612
  64.7 10.0 %copy-start.5 = (f32[64,256]{1,0:T(8,128)}, f32[64,256]{1,0:T(8,128)S(1)}, u32[]{:S(2)}) copy-start(f32[64,256]{1,0:T(8,128)S(1)} %slice_bitcast_fusion.1) | copy-start | bytes 196612
  67.9 8.8 %copy-start = (f32[3,1,68,256]{3,2,1,0:T(8,128)}, f32[3,1,68,256]{3,2,1,0:T(8,128)S(1)}, u32[]{:S(2)}) copy-start(f32[3,1,68,256]{3,2,1,0:T(8,128)S(1)} %collective-permute-done.2) | copy-start | bytes 626692
  68.1 6.6 %copy-start.26 = (f32[16,256]{1,0:T(8,128)}, f32[16,256]{1,0:T(8,128)S(1)}, u32[]{:S(2)}) copy-start(f32[16,256]{1,0:T(8,128)S(1)} %get-tuple-element.93) | copy-start | bytes 49156
  68.1 6.6 %copy-start.28 = (f32[16,256]{1,0:T(8,128)}, f32[16,256]{1,0:T(8,128)S(1)}, u32[]{:S(2)}) copy-start(f32[16,256]{1,0:T(8,128)S(1)} %get-tuple-element.92) | copy-start | bytes 49156
  68.1 6.6 %copy-start.30 = (f32[16,256]{1,0:T(8,128)}, f32[16,256]{1,0:T(8,128)S(1)}, u32[]{:S(2)}) copy-start(f32[16,256]{1,0:T(8,128)S(1)} %get-tuple-element.91) | copy-start | bytes 49156
  68.1 9.7 %copy-start.18 = (f32[16,256]{1,0:T(8,128)}, f32[16,256]{1,0:T(8,128)S(1)}, u32[]{:S(2)}) copy-start(f32[16,256]{1,0:T(8,128)S(1)} %get-tuple-element.90) | copy-start | bytes 49156
  70.6 6.1 %copy-start.20 = (f32[16,256]{1,0:T(8,128)}, f32[16,256]{1,0:T(8,128)S(1)}, u32[]{:S(2)}) copy-start(f32[16,256]{1,0:T(8,128)S(1)} %get-tuple-element.98) | copy-start | bytes 49156
  70.6 6.1 %copy-start.22 = (f32[16,256]{1,0:T(8,128)}, f32[16,256]{1,0:T(8,128)S(1)}, u32[]{:S(2)}) copy-start(f32[16,256]{1,0:T(8,128)S(1)} %get-tuple-element.97) | copy-start | bytes 49156
  70.6 6.1 %copy-start.24 = (f32[16,256]{1,0:T(8,128)}, f32[16,256]{1,0:T(8,128)S(1)}, u32[]{:S(2)}) copy-start(f32[16,256]{1,0:T(8,128)S(1)} %get-tuple-element.96) | copy-start | bytes 49156
  70.6 6.1 %copy-start.16 = (f32[16,256]{1,0:T(8,128)}, f32[16,256]{1,0:T(8,128)S(1)}, u32[]{:S(2)}) copy-start(f32[16,256]{1,0:T(8,128)S(1)} %get-tuple-element.95) | copy-start | bytes 49156
  70.6 6.1 %copy-start.3 = (f32[64,256]{1,0:T(8,128)}, f32[64,256]{1,0:T(8,128)S(1)}, u32[]{:S(2)}) copy-start(f32[64,256]{1,0:T(8,128)S(1)} %get-tuple-element.79) | copy-start | bytes 196612
  70.7 7.1 %copy-start.1 = (f32[64,256]{1,0:T(8,128)}, f32[64,256]{1,0:T(8,128)S(1)}, u32[]{:S(2)}) copy-start(f32[64,256]{1,0:T(8,128)S(1)} %get-tuple-element.67) | copy-start | bytes 196612
  79.8 27.8 %copy-start.34 = (f32[16]{0:T(128)S(1)}, f32[16]{0:T(128)}, u32[]{:S(2)}) copy-start(f32[16]{0:T(128)} %sqrt.7) | copy-start | bytes 196
  79.8 28.6 %copy-start.31 = (f32[16,256]{1,0:T(8,128)S(1)}, f32[16,256]{1,0:T(8,128)}, u32[]{:S(2)}) copy-start(f32[16,256]{1,0:T(8,128)} %copy-done.30) | copy-start | bytes 49156
  107.5 6.6 %copy-start.13 = (f32[64,256]{1,0:T(8,128)S(1)}, f32[64,256]{1,0:T(8,128)}, u32[]{:S(2)}) copy-start(f32[64,256]{1,0:T(8,128)} %copy-done.12) | copy-start | bytes 196612
  107.6 6.6 %copy-start.27 = (f32[16,256]{1,0:T(8,128)S(1)}, f32[16,256]{1,0:T(8,128)}, u32[]{:S(2)}) copy-start(f32[16,256]{1,0:T(8,128)} %copy-done.26) | copy-start | bytes 49156
  107.6 8.6 %copy-start.2 = (f32[64,256]{1,0:T(8,128)S(1)}, f32[64,256]{1,0:T(8,128)}, u32[]{:S(2)}) copy-start(f32[64,256]{1,0:T(8,128)} %copy-done.1) | copy-start | bytes 196612
  107.6 8.6 %copy-start.19 = (f32[16,256]{1,0:T(8,128)S(1)}, f32[16,256]{1,0:T(8,128)}, u32[]{:S(2)}) copy-start(f32[16,256]{1,0:T(8,128)} %copy-done.18) | copy-start | bytes 49156
  107.6 10.0 %copy-start.11 = (f32[64,256]{1,0:T(8,128)S(1)}, f32[64,256]{1,0:T(8,128)}, u32[]{:S(2)}) copy-start(f32[64,256]{1,0:T(8,128)} %copy-done.10) | copy-start | bytes 196612
  107.6 10.0 %copy-start.25 = (f32[16,256]{1,0:T(8,128)S(1)}, f32[16,256]{1,0:T(8,128)}, u32[]{:S(2)}) copy-start(f32[16,256]{1,0:T(8,128)} %copy-done.24) | copy-start | bytes 49156
  107.6 12.0 %copy-start.6 = (f32[64,256]{1,0:T(8,128)S(1)}, f32[64,256]{1,0:T(8,128)}, u32[]{:S(2)}) copy-start(f32[64,256]{1,0:T(8,128)} %copy-done.5) | copy-start | bytes 196612
  107.6 12.0 %copy-start.23 = (f32[16,256]{1,0:T(8,128)S(1)}, f32[16,256]{1,0:T(8,128)}, u32[]{:S(2)}) copy-start(f32[16,256]{1,0:T(8,128)} %copy-done.22) | copy-start | bytes 49156
  108.4 12.6 %copy-start.9 = (f32[64,256]{1,0:T(8,128)S(1)}, f32[64,256]{1,0:T(8,128)}, u32[]{:S(2)}) copy-start(f32[64,256]{1,0:T(8,128)} %copy-done.8) | copy-start | bytes 196612
  108.4 12.6 %copy-start.21 = (f32[16,256]{1,0:T(8,128)S(1)}, f32[16,256]{1,0:T(8,128)}, u32[]{:S(2)}) copy-start(f32[16,256]{1,0:T(8,128)} %copy-done.20) | copy-start | bytes 49156
  110.7 12.7 %copy-start.35 = (f32[16]{0:T(128)S(1)}, f32[16]{0:T(128)}, u32[]{:S(2)}) copy-start(f32[16]{0:T(128)} %sqrt.7) | copy-start | bytes 196
  (10 other events, 42.9 us)
where the time goes:
time: 166 us; the launch traced here: 164 us
  matrix products  52.5 us (32%)
  blocking collectives  36 us (22%)
  waiting for transfers between devices  33.6 us (20%)
  starting transfers between devices  26.4 us (16%)
  local copies, waits for them, and re-layouts  11.3 us (7%)
  between operations  2.18 us (1%)
    all_to_all x1, blocking collectives, local(): lax.all_to_all(analysed, 'mem', split_axis=0, concat_axis=2, tiled=True)  36 us
    all_to_all x1, waiting for transfers between devices, local(): lax.all_to_all(state, 'mem', split_axis=2, concat_axis=0, tiled=True)  26.7 us
    dot_general x9, matrix products, transforms(): jnp.einsum('bko,o->bk', weighted, innovation, precision=highest)  15.1 us
    all_to_all x1, starting transfers between devices, local(): lax.all_to_all(state, 'mem', split_axis=2, concat_axis=0, tiled=True)  14.8 us
    dot_general x10, matrix products, newton_step(): jnp.einsum('bij,bjk->bik', upper_iter, factor, precision=highest)  10.1 us
    dot_general x10, matrix products, newton_step(): jnp.einsum('bij,bjk->bik', lower_iter, upper_iter, precision=highest)  9.62 us
    dot_general x9, matrix products, transforms(): jnp.einsum('bko,jo->bkj', weighted, spread, precision=highest)  8.92 us
    ppermute x2, starting transfers between devices, extended(): lax.ppermute(tail, axis, [(i, (i + 1) % count) for i in range(ends)])  8.31 us
  transfers between devices with their start and end apart: 5, of which 4 were waited for; matrix products, arithmetic and copies ran while one was open for 0% of the time, Pallas kernels for 0%

commit v1 on v0

v1 whole, which is shorter than its diff:
```python
import functools

import jax
import jax.numpy as jnp
from jax import lax
from jax.experimental import pallas as pl
from jax.experimental.pallas import tpu as pltpu
from jax.sharding import PartitionSpec as P

K = 64
LEV = 2
ROWS = 128
COLS = 32
BLK = 16
OBS = 256
NSI = 10
N_MEM = 64
N_GY = 8
NR = ROWS // BLK
OWN = 4
GRAM_ROWS = NR * K + 16

MESH = pl.DeviceIdType.MESH
f32 = jnp.float32
bf16 = jnp.bfloat16

SIDES = [(dx, dy) for dx in (-1, 0, 1) for dy in (-1, 0, 1) if (dx, dy) != (0, 0)]


def split(x):
    hi = x.astype(bf16)
    lo = (x - hi.astype(f32)).astype(bf16)
    return hi, lo


def dot(a, b):
    return jnp.dot(a, b, preferred_element_type=f32)


def dot_nt(a, b):
    return lax.dot_general(a, b, (((1,), (1,)), ((), ())), preferred_element_type=f32)


def peer(me, step):
    j = step % 8
    r = step // 8
    dz = ((j + 1) // 2 * (2 * (j % 2) - 1) + 8) % 8
    dx = r // 2
    dc = r % 2
    z, x, c = me // 8, me // 2 % 4, me % 2
    target = (z + dz) % 8 * 8 + (x + dx) % 4 * 2 + (c + dc) % 2
    source = (z + 8 - dz) % 8 * 8 + (x + 4 - dx) % 4 * 2 + (c + 2 - dc) % 2
    return target, source


def kernel(
    state_ref, meta_ref, out_ref,
    tile_ref, mixed_ref, ens_ref, halo_ref, z_ref, o_ref, gram_ref,
    own_sem, in_send, in_recv, meta_send, meta_recv, ens_send, ens_recv, out_send, out_recv,
):
    me = lax.axis_index("mem")
    gy = lax.axis_index("gy")
    barrier = pltpu.get_barrier_semaphore()

    def greet(step, _):
        target, _source = peer(me, step)
        pl.semaphore_signal(barrier, inc=1, device_id=(target, gy), device_id_type=MESH)
        return 0

    lax.fori_loop(1, N_MEM, greet, 0)
    for dx, dy in SIDES:
        if dy != 0:
            device = ((me + dx + N_MEM) % N_MEM, (gy + dy + N_GY) % N_GY)
            pl.semaphore_signal(barrier, inc=1, device_id=device, device_id_type=MESH)
    pl.semaphore_wait(barrier, N_MEM - 1 + 6)

    def entry_copy(target, slot):
        return pltpu.make_async_remote_copy(
            src_ref=state_ref.at[0, :, pl.ds(pl.multiple_of(target * COLS, COLS), COLS), :],
            dst_ref=tile_ref.at[slot],
            send_sem=in_send.at[target],
            recv_sem=in_recv.at[slot],
            device_id=(target, gy),
            device_id_type=MESH,
        )

    def side_copy(src, dst, send, recv, index):
        dx, dy = SIDES[index]
        slot = (dx + 1) * 3 + dy + 1
        device = ((me - dx + N_MEM) % N_MEM, (gy - dy + N_GY) % N_GY)
        return pltpu.make_async_remote_copy(
            src_ref=src,
            dst_ref=dst.at[slot],
            send_sem=send.at[index],
            recv_sem=recv.at[index],
            device_id=device,
            device_id_type=MESH,
        )

    meta_copies = [side_copy(meta_ref, halo_ref, meta_send, meta_recv, i) for i in range(8)]
    for copy in meta_copies:
        copy.start()

    def start_entry(step, _):
        target, _source = peer(me, step)
        entry_copy(target, me).start()
        return 0

    lax.fori_loop(1, N_MEM, start_entry, 0)
    own_in = pltpu.make_async_copy(
        state_ref.at[0, :, pl.ds(pl.multiple_of(me * COLS, COLS), COLS), :],
        tile_ref.at[me],
        own_sem.at[0],
    )
    own_in.start()
    halo_ref[OWN] = meta_ref[...]
    own_in.wait()

    def finish_entry(step, _):
        target, source = peer(me, step)
        entry_copy(target, source).wait()
        return 0

    lax.fori_loop(1, N_MEM, finish_entry, 0)

    meta = meta_ref[...]
    pick_row = (
        lax.broadcasted_iota(jnp.int32, (ROWS, OBS), 0).astype(f32) == meta[3:4]
    ).astype(f32).astype(bf16)
    pick_col = lax.broadcasted_iota(jnp.int32, (LEV * COLS, OBS), 0).astype(f32) == meta[4:5]

    def observe(group, _):
        first = pl.multiple_of(group * 16, 16)
        cells = tile_ref[pl.ds(first, 16)].reshape(16 * LEV * COLS, ROWS)
        rows = dot(cells, pick_row).reshape(16, LEV * COLS, OBS)
        seen = jnp.sum(jnp.where(pick_col[None], rows, 0.0), axis=1)
        ens_ref[OWN, pl.ds(first, 16), :] = seen.astype(bf16)
        return 0

    lax.fori_loop(0, K // 16, observe, 0)

    ens_copies = [side_copy(ens_ref.at[OWN], ens_ref, ens_send, ens_recv, i) for i in range(8)]
    for copy in ens_copies:
        copy.start()
    for copy in meta_copies:
        copy.wait()
    for copy in ens_copies:
        copy.wait()

    left = lax.broadcasted_iota(jnp.int32, (K, 2 * K), 1) < K
    left_row = lax.broadcasted_iota(jnp.int32, (1, 2 * K), 1) < K
    lane = lax.broadcasted_iota(jnp.int32, (K, 2 * K), 1)
    eye = (lane % K == lax.broadcasted_iota(jnp.int32, (K, 2 * K), 0)).astype(f32)
    left_bf = jnp.where(left, 1.0, 0.0).astype(bf16)
    right_bf = jnp.where(left, 0.0, 1.0).astype(bf16)
    i_row = lax.broadcasted_iota(jnp.int32, (256, 256), 0)
    i_col = lax.broadcasted_iota(jnp.int32, (256, 256), 1)
    swap = jnp.where(
        (i_row // 16 == i_col % 16) & (i_row % 16 == i_col // 16), 1.0, 0.0
    ).astype(bf16)
    reach_sq = meta[5:6] * meta[5:6]
    centre_r = lax.broadcasted_iota(jnp.int32, (NR, OBS), 0).astype(f32) * BLK + (BLK - 1) / 2.0
    row_group = lax.broadcasted_iota(jnp.int32, (K, 2 * ROWS), 1) % ROWS // BLK
    group_masks = [jnp.where(row_group == r, 1.0, 0.0).astype(bf16) for r in range(NR)]

    def halves_sum(x):
        total = jnp.sum(x, axis=1, keepdims=True)
        first = jnp.sum(jnp.where(left, x, 0.0), axis=1, keepdims=True)
        return jnp.where(left, first, total - first)

    def halves_sum_exact(x):
        first = jnp.sum(jnp.where(left, x, 0.0), axis=1, keepdims=True)
        second = jnp.sum(jnp.where(left, 0.0, x), axis=1, keepdims=True)
        return jnp.where(left, first, second)

    def weighted(slot, dx, dy, a):
        ens = ens_ref[slot].astype(f32)
        about = halo_ref[slot]
        centre = jnp.sum(ens, axis=0, keepdims=True) * (1.0 / K)
        spread = ens - centre
        innovation = about[1:2] - centre
        inside = (me + dx >= 0) & (me + dx < N_MEM) & (gy + dy >= 0) & (gy + dy < N_GY)
        weight = about[0:1] * jnp.where(inside, 1.0, 0.0)
        centre_c = (a * BLK).astype(f32) + (BLK - 1) / 2.0
        gap_c = (dx * COLS) * 1.0 + about[2:3] - centre_c
        gap_r = (dy * ROWS) * 1.0 + about[3:4] - centre_r
        taper = jnp.square(jnp.maximum(1.0 - (gap_c * gap_c + gap_r * gap_r) / reach_sq, 0.0))
        rho = taper * weight
        drive = jnp.concatenate([rho * innovation, jnp.zeros((8, OBS), f32)], axis=0)
        hi, lo = split(spread)
        return rho, spread, drive, jnp.concatenate([hi, lo], axis=0)

    def product(parts, both):
        hi, lo = split(jnp.concatenate(parts, axis=0))
        return dot_nt(hi, both) + dot_nt(lo, both)

    def band(a, _):
        dx = 2 * a - 1
        side = 6 * a + 1
        rho, spread, drive, both = weighted(OWN, 0, 0, a)
        gram_ref[...] = product([rho[r : r + 1] * spread for r in range(NR)] + [drive], both)
        rho, spread, drive, both = weighted(side, dx, 0, a)
        gram_ref[...] += product([rho[r : r + 1] * spread for r in range(NR)] + [drive], both)
        for dy, r in ((-1, 0), (1, NR - 1)):
            for slot, step in ((OWN + dy, 0), (side + dy, dx)):
                rho, spread, drive, both = weighted(slot, step, dy, a)
                part = product([rho[r : r + 1] * spread, drive], both)
                gram_ref[r * K : (r + 1) * K, :] += part[:K]
                gram_ref[NR * K :, :] += part[K:]

        def folded(block):
            return block + pltpu.roll(block, K, 1)

        drives = folded(gram_ref[NR * K :, :])
        uppers, lowers, scales, drive_rows = [], [], [], []
        for pair in range(NR // 2):
            r = 2 * pair
            first = folded(gram_ref[r * K : (r + 1) * K, :])
            second = folded(gram_ref[(r + 1) * K : (r + 2) * K, :])
            system = (K - 1.0) * eye + jnp.where(left, first, second)
            diagonal = jnp.sum(system * eye, axis=0, keepdims=True)
            trace_l = jnp.sum(jnp.where(left_row, diagonal, 0.0), axis=1, keepdims=True)
            trace_r = jnp.sum(jnp.where(left_row, 0.0, diagonal), axis=1, keepdims=True)
            scale = jnp.where(left_row, trace_l, trace_r)
            scales.append(scale)
            drive_rows.append(jnp.where(left_row, drives[r : r + 1], drives[r + 1 : r + 2]))
            uppers.append(system / scale)

        def diag_rhs(hi, lo):
            def blocks(x):
                return jnp.concatenate([x * left_bf, x * right_bf], axis=0)

            return blocks(hi), blocks(lo)

        def times(hi, lo, rhs):
            rhs_hi, rhs_lo = rhs
            return dot(
                jnp.concatenate([hi, lo], axis=1), jnp.concatenate([rhs_hi, rhs_hi], axis=0)
            ) + dot(hi, rhs_lo)

        next_uppers = []
        for upper in uppers:
            hi, lo = split(upper)
            next_uppers.append(1.5 * upper - 0.5 * times(hi, lo, diag_rhs(hi, lo)))
            lowers.append(1.5 * eye - 0.5 * upper)

        def sweep(_, carry):
            cur_uppers, cur_lowers = carry
            new_uppers, new_lowers = [], []
            for upper, lower in zip(cur_uppers, cur_lowers):
                upper_hi, upper_lo = split(upper)
                lower_hi, lower_lo = split(lower)
                near = times(lower_hi, lower_lo, diag_rhs(upper_hi, upper_lo))
                near_hi, near_lo = split(near)
                stacked = times(
                    jnp.concatenate([upper_hi, lower_hi], axis=0),
                    jnp.concatenate([upper_lo, lower_lo], axis=0),
                    diag_rhs(near_hi, near_lo),
                )
                new_uppers.append(1.5 * upper - 0.5 * stacked[:K])
                new_lowers.append(1.5 * lower - 0.5 * stacked[K:])
            return tuple(new_uppers), tuple(new_lowers)

        uppers, lowers = lax.fori_loop(1, NSI - 1, sweep, (tuple(next_uppers), tuple(lowers)))

        mixings = []
        for pair in range(NR // 2):
            upper, lower = uppers[pair], lowers[pair]
            upper_hi, upper_lo = split(upper)
            lower_hi, lower_lo = split(lower)
            near = times(lower_hi, lower_lo, diag_rhs(upper_hi, upper_lo))
            lower = 1.5 * lower - 0.5 * times(lower_hi, lower_lo, diag_rhs(*split(near)))
            inv_root = lower / jnp.sqrt(scales[pair])
            half = halves_sum_exact(inv_root * drive_rows[pair])
            shift = jnp.sum(half * inv_root, axis=0, keepdims=True)
            transform = (K - 1.0) ** 0.5 * inv_root + shift
            mean = halves_sum_exact(transform) * (1.0 / K)
            mixings.append((1.0 / K + transform - mean).astype(bf16))
        mix_lo = jnp.concatenate(mixings[:2], axis=1)
        mix_hi = jnp.concatenate(mixings[2:], axis=1)

        first_col = pl.multiple_of(a * BLK, BLK)
        for group in range(K // 16):
            members = pl.ds(group * 16, 16)
            cells = jnp.concatenate(
                [
                    tile_ref[members, lev, pl.ds(first_col, BLK), :].reshape(256, ROWS)
                    for lev in range(LEV)
                ],
                axis=1,
            )
            z_ref[:, members, :] = dot(swap, cells).astype(bf16).reshape(16, 16, 2 * ROWS)

        def mix_column(c, _):
            cells = z_ref[c]
            low = jnp.concatenate([cells * m for m in group_masks[:4]], axis=0)
            high = jnp.concatenate([cells * m for m in group_masks[4:]], axis=0)
            o_ref[c] = (dot(mix_lo, low) + dot(mix_hi, high)).astype(bf16)
            return 0

        lax.fori_loop(0, BLK, mix_column, 0, unroll=4)

        for group in range(K // 16):
            members = pl.ds(group * 16, 16)
            cells = dot(swap, o_ref[:, members, :].reshape(256, 2 * ROWS)).astype(bf16)
            for lev in range(LEV):
                mixed_ref[members, lev, pl.ds(first_col, BLK), :] = cells[
                    :, lev * ROWS : (lev + 1) * ROWS
                ].reshape(16, BLK, ROWS)

        def start_exit(step, _):
            target, _source = peer(me, step)
            exit_copy(a, target, me).start()
            return 0

        lax.fori_loop(1, N_MEM, start_exit, 0)
        own_exit(a).start()
        return 0

    def exit_copy(a, target, owner):
        return pltpu.make_async_remote_copy(
            src_ref=mixed_ref.at[target, :, pl.ds(pl.multiple_of(a * BLK, BLK), BLK), :],
            dst_ref=out_ref.at[
                0, :, pl.ds(pl.multiple_of(owner * COLS + a * BLK, BLK), BLK), :
            ],
            send_sem=out_send.at[a, target],
            recv_sem=out_recv.at[a, owner],
            device_id=(target, gy),
            device_id_type=MESH,
        )

    def own_exit(a):
        return pltpu.make_async_copy(
            mixed_ref.at[me, :, pl.ds(pl.multiple_of(a * BLK, BLK), BLK), :],
            out_ref.at[0, :, pl.ds(pl.multiple_of(me * COLS + a * BLK, BLK), BLK), :],
            own_sem.at[1 + a],
        )

    lax.fori_loop(0, 2, band, 0)

    for a in range(2):
        own_exit(a).wait()

        def finish_exit(step, _):
            target, source = peer(me, step)
            exit_copy(a, target, source).wait()
            return 0

        lax.fori_loop(1, N_MEM, finish_exit, 0)


def local(state, obs_index, obs_count, obs_value, obs_var, radius):
    slots = obs_index[0]
    live = lax.broadcasted_iota(jnp.int32, (1, OBS), 1) < obs_count
    weight = jnp.where(live, 1.0 / obs_var[0], 0.0)
    meta = jnp.concatenate(
        [
            weight,
            obs_value[0],
            (slots // ROWS % COLS).astype(f32),
            (slots % ROWS).astype(f32),
            (slots // ROWS).astype(f32),
            jnp.broadcast_to(radius, (1, OBS)).astype(f32),
            jnp.zeros((2, OBS), f32),
        ],
        axis=0,
    )
    dma = pltpu.SemaphoreType.DMA
    return pl.pallas_call(
        kernel,
        out_shape=jax.ShapeDtypeStruct(state.shape, bf16),
        in_specs=[pl.BlockSpec(memory_space=pl.ANY), pl.BlockSpec(memory_space=pltpu.VMEM)],
        out_specs=pl.BlockSpec(memory_space=pl.ANY),
        scratch_shapes=[
            pltpu.VMEM((K, LEV, COLS, ROWS), bf16),
            pltpu.VMEM((K, LEV, COLS, ROWS), bf16),
            pltpu.VMEM((9, K, OBS), bf16),
            pltpu.VMEM((9, 8, OBS), f32),
            pltpu.VMEM((BLK, K, LEV * ROWS), bf16),
            pltpu.VMEM((BLK, K, LEV * ROWS), bf16),
            pltpu.VMEM((GRAM_ROWS, 2 * K), f32),
            dma((3,)),
            dma((N_MEM,)),
            dma((N_MEM,)),
            dma((8,)),
            dma((8,)),
            dma((8,)),
            dma((8,)),
            dma((2, N_MEM)),
            dma((2, N_MEM)),
        ],
        compiler_params=pltpu.CompilerParams(collective_id=0, has_side_effects=True),
    )(state, meta)


def solution(mesh):
    in_specs = (
        P("mem", None, None, "gy"),
        P("mem", "gy", None),
        P("mem", "gy"),
        P("mem", "gy", None),
        P("mem", "gy", None),
        P("mem", "gy"),
    )
    out_specs = P("mem", None, None, "gy")
    return jax.shard_map(local, mesh=mesh, in_specs=in_specs, out_specs=out_specs, check_vma=False)
```

time: 166 us -> 101 us (0.61)
  Pallas kernels: 0 us -> 94.1 us
  matrix products: 52.5 us -> 0 us
  blocking collectives: 36 us -> 0 us
  waiting for transfers between devices: 33.6 us -> 0 us
  starting transfers between devices: 26.4 us -> 0 us
  local copies, waits for them, and re-layouts: 11.3 us -> 4.89 us
    pallas_call x0 -> x1, Pallas kernels: none -> 94.1 us  [local(): pl.pallas_call(kernel, out_shape=jax.ShapeDtypeStruct(state.shape, bf16),...]
    dot_general x51 -> x0, matrix products: 52.5 us -> none  [the longest x9 15.1 us: transforms(): jnp.einsum('bko,o->bk', weighted, innovation, precision=highest)]
    all_to_all x1 -> x0, blocking collectives: 36 us -> none  [local(): lax.all_to_all(analysed, 'mem', split_axis=0, concat_axis=2, tiled=True)]
    all_to_all x1 -> x0, waiting for transfers between devices: 26.7 us -> none  [local(): lax.all_to_all(state, 'mem', split_axis=2, concat_axis=0, tiled=True)]
    all_to_all x1 -> x0, starting transfers between devices: 14.8 us -> none  [local(): lax.all_to_all(state, 'mem', split_axis=2, concat_axis=0, tiled=True)]
    ppermute x4 -> x0, starting transfers between devices: 11.5 us -> none  [the longest x2 8.31 us: extended(): lax.ppermute(tail, axis, [(i, (i + 1) % count) for i in range(ends)])]
    ppermute x4 -> x0, waiting for transfers between devices: 6.91 us -> none  [the longest x2 5.16 us: extended(): lax.ppermute(head, axis, [((i + 1) % count, i) for i in range(ends)])]
    all_to_all x3 -> x0, local copies, waits for them, and re-layouts: 2.65 us -> none  [the longest x2 1.6 us: local(): lax.all_to_all(state, 'mem', split_axis=2, concat_axis=0, tiled=True)]
  transfers between devices with their start and end apart: 5 -> 0, of which waited for: 4 -> 0; matrix products, arithmetic and copies ran while one was open for 0% -> 0% of each run, Pallas kernels for 0% -> 0%
where the time goes in v1:
time: 101 us; the launch traced here: 100 us
  Pallas kernels  94.1 us (93%)
  local copies, waits for them, and re-layouts  4.89 us (5%)
  between operations  1.35 us (1%)
    pallas_call x1, Pallas kernels, local(): pl.pallas_call(kernel, out_shape=jax.ShapeDtypeStruct(state.shape, bf16),...  94.1 us
    unnamed x7, local copies, waits for them, and re-layouts  4.26 us

profile of v1, /device:TPU:1, one launch (start us, length us, event | category | flops | bytes accessed | tf_op | source)
XLA Modules:
  0.0 100.4 jit_solution(10950783334900393983)
XLA Ops:
  1.3 0.0 copy-start.1
  1.3 0.7 copy-done.1
  2.0 0.0 copy-start.2
  2.0 0.7 copy-done.2
  2.7 0.0 copy-start
  2.7 0.7 copy-done
  3.4 0.6 concatenate.3.meta_ref
  4.0 94.1 %shard_map.64 = bf16[1,2,2048,128]{3,2,1,0:T(8,128)(2,1)} custom-call(bf16[1,2,2048,128]{3,2,1,0:T(8,128)(2,1)} %state_ref.1, f32[8,256]{1,0:T(8,128)} %concatenate.3.meta_ref), custom_call_target="tpu_custom_call" | custom-call | tf_op jit(solution)/shard_map/pallas_call | solution.py:369
  98.1 2.3 %copy.10 = bf16[1,2,2048,128]{3,2,1,0:T(8,128)(2,1)} copy(bf16[1,2,2048,128]{3,2,1,0:T(8,128)(2,1)} %shard_map.64) | data formatting | bytes 2097152
  (5 shorter events, 0.0 us)
Async XLA Ops:
  1.3 0.7 copy-start.1
  2.0 0.7 copy-start.2
  2.7 0.7 copy-start

commit v2 on v1

--- a/solution.py
+++ b/solution.py
@@ -41,20 +41,34 @@
     return lax.dot_general(a, b, (((1,), (1,)), ((), ())), preferred_element_type=f32)
 
 
-def peer(me, step):
-    j = step % 8
-    r = step // 8
-    dz = ((j + 1) // 2 * (2 * (j % 2) - 1) + 8) % 8
-    dx = r // 2
-    dc = r % 2
-    z, x, c = me // 8, me // 2 % 4, me % 2
-    target = (z + dz) % 8 * 8 + (x + dx) % 4 * 2 + (c + dc) % 2
-    source = (z + 8 - dz) % 8 * 8 + (x + 4 - dx) % 4 * 2 + (c + 2 - dc) % 2
-    return target, source
+def rem(a, b):
+    return lax.rem(a, jnp.int32(b))
+
+
+def peers_of(me):
+    z, x, c = lax.div(me, jnp.int32(8)), rem(lax.div(me, jnp.int32(2)), 4), rem(me, 2)
+    planes = [rem(z + d, 8) * 8 for d in range(8)]
+    order = [0, 1, 7, 2, 6, 3, 5, 4]
+
+    def each(fn):
+        for dz in order[1:]:
+            fn(planes[dz] + x * 2 + c, planes[8 - dz] + x * 2 + c)
+
+        def row(r, _):
+            dx, dc = lax.div(r, jnp.int32(2)), rem(r, 2)
+            there = rem(x + dx, 4) * 2 + rem(c + dc, 2)
+            back = rem(x + 4 - dx, 4) * 2 + rem(c + 2 - dc, 2)
+            for dz in order:
+                fn(planes[dz] + there, planes[(8 - dz) % 8] + back)
+            return 0
+
+        lax.fori_loop(1, 8, row, 0)
+
+    return each
 
 
 def kernel(
-    state_ref, meta_ref, out_ref,
+    state_ref, index_ref, count_ref, value_ref, var_ref, radius_ref, out_ref,
     tile_ref, mixed_ref, ens_ref, halo_ref, z_ref, o_ref, gram_ref,
     own_sem, in_send, in_recv, meta_send, meta_recv, ens_send, ens_recv, out_send, out_recv,
 ):
@@ -62,16 +76,34 @@
     gy = lax.axis_index("gy")
     barrier = pltpu.get_barrier_semaphore()
 
-    def greet(step, _):
-        target, _source = peer(me, step)
+    each_peer = peers_of(me)
+
+    def greet(target, _source):
         pl.semaphore_signal(barrier, inc=1, device_id=(target, gy), device_id_type=MESH)
-        return 0
-
-    lax.fori_loop(1, N_MEM, greet, 0)
+
+    each_peer(greet)
     for dx, dy in SIDES:
         if dy != 0:
-            device = ((me + dx + N_MEM) % N_MEM, (gy + dy + N_GY) % N_GY)
+            device = (rem(me + dx + N_MEM, N_MEM), rem(gy + dy + N_GY, N_GY))
             pl.semaphore_signal(barrier, inc=1, device_id=device, device_id_type=MESH)
+
+    slots = index_ref[0]
+    live = lax.broadcasted_iota(jnp.int32, (1, OBS), 1) < count_ref[0, 0]
+    cell = lax.div(slots, jnp.int32(ROWS))
+    meta = jnp.concatenate(
+        [
+            jnp.where(live, 1.0 / var_ref[0], 0.0),
+            value_ref[0],
+            rem(cell, COLS).astype(f32),
+            rem(slots, ROWS).astype(f32),
+            cell.astype(f32),
+            jnp.zeros((3, OBS), f32),
+        ],
+        axis=0,
+    )
+    halo_ref[OWN] = meta
+    radius = jnp.full((1, OBS), radius_ref[0, 0], jnp.int32).astype(f32)
+    reach_sq = radius * radius
     pl.semaphore_wait(barrier, N_MEM - 1 + 6)
 
     def entry_copy(target, slot):
@@ -87,7 +119,7 @@
     def side_copy(src, dst, send, recv, index):
         dx, dy = SIDES[index]
         slot = (dx + 1) * 3 + dy + 1
-        device = ((me - dx + N_MEM) % N_MEM, (gy - dy + N_GY) % N_GY)
+        device = (rem(me - dx + N_MEM, N_MEM), rem(gy - dy + N_GY, N_GY))
         return pltpu.make_async_remote_copy(
             src_ref=src,
             dst_ref=dst.at[slot],
@@ -97,33 +129,21 @@
             device_id_type=MESH,
         )
 
-    meta_copies = [side_copy(meta_ref, halo_ref, meta_send, meta_recv, i) for i in range(8)]
+    meta_copies = [side_copy(halo_ref.at[OWN], halo_ref, meta_send, meta_recv, i) for i in range(8)]
     for copy in meta_copies:
         copy.start()
 
-    def start_entry(step, _):
-        target, _source = peer(me, step)
-        entry_copy(target, me).start()
-        return 0
-
-    lax.fori_loop(1, N_MEM, start_entry, 0)
+    each_peer(lambda target, _source: entry_copy(target, me).start())
     own_in = pltpu.make_async_copy(
         state_ref.at[0, :, pl.ds(pl.multiple_of(me * COLS, COLS), COLS), :],
         tile_ref.at[me],
         own_sem.at[0],
     )
     own_in.start()
-    halo_ref[OWN] = meta_ref[...]
     own_in.wait()
 
-    def finish_entry(step, _):
-        target, source = peer(me, step)
-        entry_copy(target, source).wait()
-        return 0
-
-    lax.fori_loop(1, N_MEM, finish_entry, 0)
-
-    meta = meta_ref[...]
+    each_peer(lambda target, source: entry_copy(target, source).wait())
+
     pick_row = (
         lax.broadcasted_iota(jnp.int32, (ROWS, OBS), 0).astype(f32) == meta[3:4]
     ).astype(f32).astype(bf16)
@@ -158,7 +178,6 @@
     swap = jnp.where(
         (i_row // 16 == i_col % 16) & (i_row % 16 == i_col // 16), 1.0, 0.0
     ).astype(bf16)
-    reach_sq = meta[5:6] * meta[5:6]
     centre_r = lax.broadcasted_iota(jnp.int32, (NR, OBS), 0).astype(f32) * BLK + (BLK - 1) / 2.0
     row_group = lax.broadcasted_iota(jnp.int32, (K, 2 * ROWS), 1) % ROWS // BLK
     group_masks = [jnp.where(row_group == r, 1.0, 0.0).astype(bf16) for r in range(NR)]
@@ -308,12 +327,7 @@
                     :, lev * ROWS : (lev + 1) * ROWS
                 ].reshape(16, BLK, ROWS)
 
-        def start_exit(step, _):
-            target, _source = peer(me, step)
-            exit_copy(a, target, me).start()
-            return 0
-
-        lax.fori_loop(1, N_MEM, start_exit, 0)
+        each_peer(lambda target, _source: exit_copy(a, target, me).start())
         own_exit(a).start()
         return 0
 
@@ -341,35 +355,22 @@
     for a in range(2):
         own_exit(a).wait()
 
-        def finish_exit(step, _):
-            target, source = peer(me, step)
-            exit_copy(a, target, source).wait()
-            return 0
-
-        lax.fori_loop(1, N_MEM, finish_exit, 0)
+        each_peer(lambda target, source: exit_copy(a, target, source).wait())
 
 
 def local(state, obs_index, obs_count, obs_value, obs_var, radius):
-    slots = obs_index[0]
-    live = lax.broadcasted_iota(jnp.int32, (1, OBS), 1) < obs_count
-    weight = jnp.where(live, 1.0 / obs_var[0], 0.0)
-    meta = jnp.concatenate(
-        [
-            weight,
-            obs_value[0],
-            (slots // ROWS % COLS).astype(f32),
-            (slots % ROWS).astype(f32),
-            (slots // ROWS).astype(f32),
-            jnp.broadcast_to(radius, (1, OBS)).astype(f32),
-            jnp.zeros((2, OBS), f32),
-        ],
-        axis=0,
-    )
     dma = pltpu.SemaphoreType.DMA
     return pl.pallas_call(
         kernel,
         out_shape=jax.ShapeDtypeStruct(state.shape, bf16),
-        in_specs=[pl.BlockSpec(memory_space=pl.ANY), pl.BlockSpec(memory_space=pltpu.VMEM)],
+        in_specs=[
+            pl.BlockSpec(memory_space=pl.ANY),
+            pl.BlockSpec(memory_space=pltpu.VMEM),
+            pl.BlockSpec(memory_space=pltpu.SMEM),
+            pl.BlockSpec(memory_space=pltpu.VMEM),
+            pl.BlockSpec(memory_space=pltpu.VMEM),
+            pl.BlockSpec(memory_space=pltpu.SMEM),
+        ],
         out_specs=pl.BlockSpec(memory_space=pl.ANY),
         scratch_shapes=[
             pltpu.VMEM((K, LEV, COLS, ROWS), bf16),
@@ -389,8 +390,10 @@
             dma((2, N_MEM)),
             dma((2, N_MEM)),
         ],
-        compiler_params=pltpu.CompilerParams(collective_id=0, has_side_effects=True),
-    )(state, meta)
+        compiler_params=pltpu.CompilerParams(
+            collective_id=0, has_side_effects=True, vmem_limit_bytes=24 * 2**20
+        ),
+    )(state, obs_index, obs_count, obs_value, obs_var, radius)
 
 
 def solution(mesh):

time: 101 us -> 93.1 us (0.922)
  Pallas kernels: 94.1 us -> 89.3 us
  local copies, waits for them, and re-layouts: 4.89 us -> 2.2 us
    pallas_call x1, Pallas kernels: 94.1 us -> 89.3 us  [local(): pl.pallas_call(kernel, out_shape=jax.ShapeDtypeStruct(state.shape, bf16),...]
    unnamed x7 -> x9, local copies, waits for them, and re-layouts: 4.26 us -> 2.2 us
where the time goes in v2:
time: 93.1 us; the launch traced here: 92.9 us
  Pallas kernels  89.3 us (96%)
  local copies, waits for them, and re-layouts  2.2 us (2%)
  between operations  1.39 us (1%)
    pallas_call x1, Pallas kernels, local(): pl.pallas_call(kernel, out_shape=jax.ShapeDtypeStruct(state.shape, bf16),...  89.3 us
    unnamed x9, local copies, waits for them, and re-layouts  2.2 us

profile of v2, /device:TPU:1, one launch (start us, length us, event | category | flops | bytes accessed | tf_op | source)
XLA Modules:
  0.0 92.9 jit_solution(8774092209645046224)
XLA Ops:
  0.0 0.0 copy-start.2
  0.0 0.0 copy-start.3
  0.7 0.0 copy-start.1
  1.4 0.0 copy-done.2
  1.4 0.0 copy-done.3
  1.4 0.0 copy-done.1
  1.4 0.0 copy-start
  1.4 1.2 %copy-done = bf16[1,2,2048,128]{3,2,1,0:T(8,128)(2,1)S(1)} copy-done((bf16[1,2,2048,128]{3,2,1,0:T(8,128)(2,1)S(1)}, bf16[1,2,2048,128]{3,2,1,0:T(8,128)(2,1)}, u32[]{:S(2)}) %copy-start) | copy-done | bytes 1048600
  2.6 89.3 %shard_map.64 = bf16[1,2,2048,128]{3,2,1,0:T(8,128)(2,1)S(1)} custom-call(bf16[1,2,2048,128]{3,2,1,0:T(8,128)(2,1)S(1)} %copy-done, s32[1,1,256]{2,1,0:T(1,128)S(1)} %copy-done.1, s32[1,1]{1,0:T(1,128)S(6)} %copy.8.count_ref, f32[1,1,256]{2,1,0:T(1,128)S(1)} %copy-done.2, f32[1,1,256]{2,1,0:T(1,128)S(1)} %copy-done.3, s32[1,1]{1,0:T(1,128)S(6)} %copy.9.radius_ref), custom_call_target="tpu_custom_call" | custom-call | tf_op jit(solution)/shard_map/pallas_call | solution.py:363
  91.9 1.0 %copy.10 = bf16[1,2,2048,128]{3,2,1,0:T(8,128)(2,1)} copy(bf16[1,2,2048,128]{3,2,1,0:T(8,128)(2,1)S(1)} %shard_map.64) | data formatting | bytes 2097152
Async XLA Ops:
  0.0 1.4 %copy-start.2 = (f32[1,1,256]{2,1,0:T(1,128)S(1)}, f32[1,1,256]{2,1,0:T(1,128)}, u32[]{:S(2)}) copy-start(f32[1,1,256]{2,1,0:T(1,128)} %value_ref.1) | copy-start | bytes 3076
  0.0 1.4 %copy-start.3 = (f32[1,1,256]{2,1,0:T(1,128)S(1)}, f32[1,1,256]{2,1,0:T(1,128)}, u32[]{:S(2)}) copy-start(f32[1,1,256]{2,1,0:T(1,128)} %var_ref.1) | copy-start | bytes 3076
  0.7 0.7 copy-start.1
  1.4 1.2 %copy-start = (bf16[1,2,2048,128]{3,2,1,0:T(8,128)(2,1)S(1)}, bf16[1,2,2048,128]{3,2,1,0:T(8,128)(2,1)}, u32[]{:S(2)}) copy-start(bf16[1,2,2048,128]{3,2,1,0:T(8,128)(2,1)} %state_ref.1) | copy-start | bytes 3145732

commit v3 on v2

--- a/solution.py
+++ b/solution.py
@@ -18,6 +18,7 @@
 N_GY = 8
 NR = ROWS // BLK
 OWN = 4
+BULK = (3, 5, 8)
 GRAM_ROWS = NR * K + 16
 
 MESH = pl.DeviceIdType.MESH
@@ -50,9 +51,10 @@
     planes = [rem(z + d, 8) * 8 for d in range(8)]
     order = [0, 1, 7, 2, 6, 3, 5, 4]
 
-    def each(fn):
-        for dz in order[1:]:
-            fn(planes[dz] + x * 2 + c, planes[8 - dz] + x * 2 + c)
+    def each(fn, first=0, last=8):
+        if first == 0:
+            for dz in order[1:]:
+                fn(planes[dz] + x * 2 + c, planes[8 - dz] + x * 2 + c)
 
         def row(r, _):
             dx, dc = lax.div(r, jnp.int32(2)), rem(r, 2)
@@ -62,15 +64,16 @@
                 fn(planes[dz] + there, planes[(8 - dz) % 8] + back)
             return 0
 
-        lax.fori_loop(1, 8, row, 0)
+        lax.fori_loop(max(first, 1), last, row, 0)
 
     return each
 
 
 def kernel(
     state_ref, index_ref, count_ref, value_ref, var_ref, radius_ref, out_ref,
-    tile_ref, mixed_ref, ens_ref, halo_ref, z_ref, o_ref, gram_ref,
-    own_sem, in_send, in_recv, meta_send, meta_recv, ens_send, ens_recv, out_send, out_recv,
+    index_all, seen_ref, raw_ref,
+    tile_ref, mixed_ref, ens_ref, halo_ref, z_ref, o_ref, gram_ref, mix_ref,
+    own_sem, index_send, index_recv, seen_send, seen_recv, in_send, in_recv, meta_send, meta_recv, ens_send, ens_recv, out_send, out_recv,
 ):
     me = lax.axis_index("mem")
     gy = lax.axis_index("gy")
@@ -88,7 +91,7 @@
             pl.semaphore_signal(barrier, inc=1, device_id=device, device_id_type=MESH)
 
     slots = index_ref[0]
-    live = lax.broadcasted_iota(jnp.int32, (1, OBS), 1) < count_ref[0, 0]
+    live = lax.broadcasted_iota(jnp.int32, (1, OBS), 1) < count_ref[...]
     cell = lax.div(slots, jnp.int32(ROWS))
     meta = jnp.concatenate(
         [
@@ -102,7 +105,7 @@
         axis=0,
     )
     halo_ref[OWN] = meta
-    radius = jnp.full((1, OBS), radius_ref[0, 0], jnp.int32).astype(f32)
+    radius = jnp.broadcast_to(radius_ref[...], (1, OBS)).astype(f32)
     reach_sq = radius * radius
     pl.semaphore_wait(barrier, N_MEM - 1 + 6)
 
@@ -129,11 +132,34 @@
             device_id_type=MESH,
         )
 
+    def index_copy(target, slot):
+        return pltpu.make_async_remote_copy(
+            src_ref=index_ref.at[0],
+            dst_ref=index_all.at[slot],
+            send_sem=index_send.at[target],
+            recv_sem=index_recv.at[slot],
+            device_id=(target, gy),
+            device_id_type=MESH,
+        )
+
+    def seen_copy(target, slot):
+        return pltpu.make_async_remote_copy(
+            src_ref=seen_ref.at[target],
+            dst_ref=raw_ref.at[slot],
+            send_sem=seen_send.at[target],
+            recv_sem=seen_recv.at[slot],
+            device_id=(target, gy),
+            device_id_type=MESH,
+        )
+
+    def start_entry(target, _source):
+        entry_copy(target, me).start()
+
+    each_peer(lambda target, _source: index_copy(target, me).start())
     meta_copies = [side_copy(halo_ref.at[OWN], halo_ref, meta_send, meta_recv, i) for i in range(8)]
     for copy in meta_copies:
         copy.start()
-
-    each_peer(lambda target, _source: entry_copy(target, me).start())
+    each_peer(start_entry, 0, BULK[0])
     own_in = pltpu.make_async_copy(
         state_ref.at[0, :, pl.ds(pl.multiple_of(me * COLS, COLS), COLS), :],
         tile_ref.at[me],
@@ -141,31 +167,32 @@
     )
     own_in.start()
     own_in.wait()
-
-    each_peer(lambda target, source: entry_copy(target, source).wait())
-
-    pick_row = (
-        lax.broadcasted_iota(jnp.int32, (ROWS, OBS), 0).astype(f32) == meta[3:4]
-    ).astype(f32).astype(bf16)
-    pick_col = lax.broadcasted_iota(jnp.int32, (LEV * COLS, OBS), 0).astype(f32) == meta[4:5]
-
-    def observe(group, _):
-        first = pl.multiple_of(group * 16, 16)
-        cells = tile_ref[pl.ds(first, 16)].reshape(16 * LEV * COLS, ROWS)
-        rows = dot(cells, pick_row).reshape(16, LEV * COLS, OBS)
-        seen = jnp.sum(jnp.where(pick_col[None], rows, 0.0), axis=1)
-        ens_ref[OWN, pl.ds(first, 16), :] = seen.astype(bf16)
+    index_all[me] = index_ref[0]
+    each_peer(lambda target, source: index_copy(target, source).wait())
+
+    row_iota = lax.broadcasted_iota(jnp.int32, (ROWS, OBS), 0)
+    cell_iota = lax.broadcasted_iota(jnp.int32, (LEV * COLS, OBS), 0)
+
+    def observe(tile, _):
+        wanted = index_all[tile]
+        pick_row = jnp.where(row_iota == (wanted & (ROWS - 1)), 1.0, 0.0).astype(bf16)
+        cells = state_ref[0, :, pl.ds(pl.multiple_of(tile * COLS, COLS), COLS), :]
+        rows = dot(cells.reshape(LEV * COLS, ROWS), pick_row)
+        picked = jnp.where(cell_iota == (wanted >> 7), rows, 0.0)
+        seen_ref[tile] = jnp.sum(picked, axis=0, keepdims=True)
         return 0
 
-    lax.fori_loop(0, K // 16, observe, 0)
-
+    lax.fori_loop(0, N_MEM, observe, 0, unroll=8)
+    raw_ref[me] = seen_ref[me]
+    each_peer(lambda target, _source: seen_copy(target, me).start())
+    each_peer(start_entry, *BULK[:2])
+    each_peer(lambda target, source: seen_copy(target, source).wait())
+
+    ens_ref[OWN] = raw_ref[:, 0, :].astype(bf16)
     ens_copies = [side_copy(ens_ref.at[OWN], ens_ref, ens_send, ens_recv, i) for i in range(8)]
     for copy in ens_copies:
         copy.start()
-    for copy in meta_copies:
-        copy.wait()
-    for copy in ens_copies:
-        copy.wait()
+    each_peer(start_entry, *BULK[1:])
 
     left = lax.broadcasted_iota(jnp.int32, (K, 2 * K), 1) < K
     left_row = lax.broadcasted_iota(jnp.int32, (1, 2 * K), 1) < K
@@ -200,7 +227,7 @@
         innovation = about[1:2] - centre
         inside = (me + dx >= 0) & (me + dx < N_MEM) & (gy + dy >= 0) & (gy + dy < N_GY)
         weight = about[0:1] * jnp.where(inside, 1.0, 0.0)
-        centre_c = (a * BLK).astype(f32) + (BLK - 1) / 2.0
+        centre_c = a * BLK + (BLK - 1) / 2.0
         gap_c = (dx * COLS) * 1.0 + about[2:3] - centre_c
         gap_r = (dy * ROWS) * 1.0 + about[3:4] - centre_r
         taper = jnp.square(jnp.maximum(1.0 - (gap_c * gap_c + gap_r * gap_r) / reach_sq, 0.0))
@@ -213,29 +240,35 @@
         hi, lo = split(jnp.concatenate(parts, axis=0))
         return dot_nt(hi, both) + dot_nt(lo, both)
 
-    def band(a, _):
+    for a in range(2):
+        rho, spread, drive, both = weighted(OWN, 0, 0, a)
+        gram_ref[a] = product([rho[r : r + 1] * spread for r in range(NR)] + [drive], both)
+    for copy in meta_copies:
+        copy.wait()
+    for copy in ens_copies:
+        copy.wait()
+
+    def folded(block):
+        return block + pltpu.roll(block, K, 1)
+
+    uppers, lowers, scales, drive_rows = [], [], [], []
+    for a in range(2):
         dx = 2 * a - 1
         side = 6 * a + 1
-        rho, spread, drive, both = weighted(OWN, 0, 0, a)
-        gram_ref[...] = product([rho[r : r + 1] * spread for r in range(NR)] + [drive], both)
         rho, spread, drive, both = weighted(side, dx, 0, a)
-        gram_ref[...] += product([rho[r : r + 1] * spread for r in range(NR)] + [drive], both)
+        gram_ref[a] += product([rho[r : r + 1] * spread for r in range(NR)] + [drive], both)
         for dy, r in ((-1, 0), (1, NR - 1)):
             for slot, step in ((OWN + dy, 0), (side + dy, dx)):
                 rho, spread, drive, both = weighted(slot, step, dy, a)
                 part = product([rho[r : r + 1] * spread, drive], both)
-                gram_ref[r * K : (r + 1) * K, :] += part[:K]
-                gram_ref[NR * K :, :] += part[K:]
-
-        def folded(block):
-            return block + pltpu.roll(block, K, 1)
-
-        drives = folded(gram_ref[NR * K :, :])
-        uppers, lowers, scales, drive_rows = [], [], [], []
+                gram_ref[a, r * K : (r + 1) * K, :] += part[:K]
+                gram_ref[a, NR * K :, :] += part[K:]
+
+        drives = folded(gram_ref[a, NR * K :, :])
         for pair in range(NR // 2):
             r = 2 * pair
-            first = folded(gram_ref[r * K : (r + 1) * K, :])
-            second = folded(gram_ref[(r + 1) * K : (r + 2) * K, :])
+            first = folded(gram_ref[a, r * K : (r + 1) * K, :])
+            second = folded(gram_ref[a, (r + 1) * K : (r + 2) * K, :])
             system = (K - 1.0) * eye + jnp.where(left, first, second)
             diagonal = jnp.sum(system * eye, axis=0, keepdims=True)
             trace_l = jnp.sum(jnp.where(left_row, diagonal, 0.0), axis=1, keepdims=True)
@@ -245,58 +278,66 @@
             drive_rows.append(jnp.where(left_row, drives[r : r + 1], drives[r + 1 : r + 2]))
             uppers.append(system / scale)
 
-        def diag_rhs(hi, lo):
-            def blocks(x):
-                return jnp.concatenate([x * left_bf, x * right_bf], axis=0)
-
-            return blocks(hi), blocks(lo)
-
-        def times(hi, lo, rhs):
-            rhs_hi, rhs_lo = rhs
-            return dot(
-                jnp.concatenate([hi, lo], axis=1), jnp.concatenate([rhs_hi, rhs_hi], axis=0)
-            ) + dot(hi, rhs_lo)
-
-        next_uppers = []
-        for upper in uppers:
-            hi, lo = split(upper)
-            next_uppers.append(1.5 * upper - 0.5 * times(hi, lo, diag_rhs(hi, lo)))
-            lowers.append(1.5 * eye - 0.5 * upper)
-
-        def sweep(_, carry):
-            cur_uppers, cur_lowers = carry
-            new_uppers, new_lowers = [], []
-            for upper, lower in zip(cur_uppers, cur_lowers):
-                upper_hi, upper_lo = split(upper)
-                lower_hi, lower_lo = split(lower)
-                near = times(lower_hi, lower_lo, diag_rhs(upper_hi, upper_lo))
-                near_hi, near_lo = split(near)
-                stacked = times(
-                    jnp.concatenate([upper_hi, lower_hi], axis=0),
-                    jnp.concatenate([upper_lo, lower_lo], axis=0),
-                    diag_rhs(near_hi, near_lo),
-                )
-                new_uppers.append(1.5 * upper - 0.5 * stacked[:K])
-                new_lowers.append(1.5 * lower - 0.5 * stacked[K:])
-            return tuple(new_uppers), tuple(new_lowers)
-
-        uppers, lowers = lax.fori_loop(1, NSI - 1, sweep, (tuple(next_uppers), tuple(lowers)))
-
-        mixings = []
-        for pair in range(NR // 2):
-            upper, lower = uppers[pair], lowers[pair]
+    def diag_rhs(hi, lo):
+        def blocks(x):
+            return jnp.concatenate([x * left_bf, x * right_bf], axis=0)
+
+        return blocks(hi), blocks(lo)
+
+    def times(hi, lo, rhs):
+        rhs_hi, rhs_lo = rhs
+        return dot(
+            jnp.concatenate([hi, lo], axis=1), jnp.concatenate([rhs_hi, rhs_hi], axis=0)
+        ) + dot(hi, rhs_lo)
+
+    next_uppers = []
+    for upper in uppers:
+        hi, lo = split(upper)
+        next_uppers.append(1.5 * upper - 0.5 * times(hi, lo, diag_rhs(hi, lo)))
+        lowers.append(1.5 * eye - 0.5 * upper)
+
+    def sweep(_, carry):
+        cur_uppers, cur_lowers = carry
+        new_uppers, new_lowers = [], []
+        for upper, lower in zip(cur_uppers, cur_lowers):
             upper_hi, upper_lo = split(upper)
             lower_hi, lower_lo = split(lower)
             near = times(lower_hi, lower_lo, diag_rhs(upper_hi, upper_lo))
-            lower = 1.5 * lower - 0.5 * times(lower_hi, lower_lo, diag_rhs(*split(near)))
-            inv_root = lower / jnp.sqrt(scales[pair])
-            half = halves_sum_exact(inv_root * drive_rows[pair])
-            shift = jnp.sum(half * inv_root, axis=0, keepdims=True)
-            transform = (K - 1.0) ** 0.5 * inv_root + shift
-            mean = halves_sum_exact(transform) * (1.0 / K)
-            mixings.append((1.0 / K + transform - mean).astype(bf16))
-        mix_lo = jnp.concatenate(mixings[:2], axis=1)
-        mix_hi = jnp.concatenate(mixings[2:], axis=1)
+            near_hi, near_lo = split(near)
+            stacked = times(
+                jnp.concatenate([upper_hi, lower_hi], axis=0),
+                jnp.concatenate([upper_lo, lower_lo], axis=0),
+                diag_rhs(near_hi, near_lo),
+            )
+            new_uppers.append(1.5 * upper - 0.5 * stacked[:K])
+            new_lowers.append(1.5 * lower - 0.5 * stacked[K:])
+        return tuple(new_uppers), tuple(new_lowers)
+
+    uppers, lowers = lax.fori_loop(1, NSI - 1, sweep, (tuple(next_uppers), tuple(lowers)))
+
+    mixings = []
+    for pair in range(NR):
+        upper, lower = uppers[pair], lowers[pair]
+        upper_hi, upper_lo = split(upper)
+        lower_hi, lower_lo = split(lower)
+        near = times(lower_hi, lower_lo, diag_rhs(upper_hi, upper_lo))
+        lower = 1.5 * lower - 0.5 * times(lower_hi, lower_lo, diag_rhs(*split(near)))
+        inv_root = lower / jnp.sqrt(scales[pair])
+        half = halves_sum_exact(inv_root * drive_rows[pair])
+        shift = jnp.sum(half * inv_root, axis=0, keepdims=True)
+        transform = (K - 1.0) ** 0.5 * inv_root + shift
+        mean = halves_sum_exact(transform) * (1.0 / K)
+        mixings.append((1.0 / K + transform - mean).astype(bf16))
+    for a in range(2):
+        for half in range(2):
+            first = 4 * a + 2 * half
+            mix_ref[a, half] = jnp.concatenate(mixings[first : first + 2], axis=1)
+
+    each_peer(lambda target, source: entry_copy(target, source).wait())
+
+    def band(a, _):
+        mix_lo = mix_ref[a, 0]
+        mix_hi = mix_ref[a, 1]
 
         first_col = pl.multiple_of(a * BLK, BLK)
         for group in range(K // 16):
@@ -363,24 +404,25 @@
     return pl.pallas_call(
         kernel,
         out_shape=jax.ShapeDtypeStruct(state.shape, bf16),
-        in_specs=[
-            pl.BlockSpec(memory_space=pl.ANY),
-            pl.BlockSpec(memory_space=pltpu.VMEM),
-            pl.BlockSpec(memory_space=pltpu.SMEM),
-            pl.BlockSpec(memory_space=pltpu.VMEM),
-            pl.BlockSpec(memory_space=pltpu.VMEM),
-            pl.BlockSpec(memory_space=pltpu.SMEM),
-        ],
+        in_specs=[pl.BlockSpec(memory_space=pltpu.VMEM)] * 6,
         out_specs=pl.BlockSpec(memory_space=pl.ANY),
         scratch_shapes=[
+            pltpu.VMEM((N_MEM, 1, OBS), jnp.int32),
+            pltpu.VMEM((N_MEM, 1, OBS), f32),
+            pltpu.VMEM((N_MEM, 1, OBS), f32),
             pltpu.VMEM((K, LEV, COLS, ROWS), bf16),
             pltpu.VMEM((K, LEV, COLS, ROWS), bf16),
             pltpu.VMEM((9, K, OBS), bf16),
             pltpu.VMEM((9, 8, OBS), f32),
             pltpu.VMEM((BLK, K, LEV * ROWS), bf16),
             pltpu.VMEM((BLK, K, LEV * ROWS), bf16),
-            pltpu.VMEM((GRAM_ROWS, 2 * K), f32),
+            pltpu.VMEM((2, GRAM_ROWS, 2 * K), f32),
+            pltpu.VMEM((2, 2, K, 4 * K), bf16),
             dma((3,)),
+            dma((N_MEM,)),
+            dma((N_MEM,)),
+            dma((N_MEM,)),
+            dma((N_MEM,)),
             dma((N_MEM,)),
             dma((N_MEM,)),
             dma((8,)),

time: 93.1 us -> 94.2 us (1.012); the launches traced: 92.9 us -> 93 us
  no operation moved by 1% of the time
where the time goes in v3:
time: 94.2 us; the launch traced here: 93 us
  Pallas kernels  89.5 us (95%)
  local copies, waits for them, and re-layouts  2.2 us (2%)
  between operations  1.39 us (1%)
    pallas_call x1, Pallas kernels, local(): pl.pallas_call(kernel, out_shape=jax.ShapeDtypeStruct(state.shape, bf16),...  89.5 us
    unnamed x9, local copies, waits for them, and re-layouts  2.2 us

profile of v3, /device:TPU:1, one launch (start us, length us, event | category | flops | bytes accessed | tf_op | source)
XLA Modules:
  0.0 93.0 jit_solution(13197429255643114618)
XLA Ops:
  0.0 0.0 copy-start.2
  0.0 0.0 copy-start.3
  0.7 0.0 copy-start.1
  1.4 0.0 copy-done.2
  1.4 0.0 copy-done.3
  1.4 0.0 copy-done.1
  1.4 0.0 copy-start
  1.4 1.2 %copy-done = bf16[1,2,2048,128]{3,2,1,0:T(8,128)(2,1)S(1)} copy-done((bf16[1,2,2048,128]{3,2,1,0:T(8,128)(2,1)S(1)}, bf16[1,2,2048,128]{3,2,1,0:T(8,128)(2,1)}, u32[]{:S(2)}) %copy-start) | copy-done | bytes 1048600
  2.6 89.5 %shard_map.64 = bf16[1,2,2048,128]{3,2,1,0:T(8,128)(2,1)S(1)} custom-call(bf16[1,2,2048,128]{3,2,1,0:T(8,128)(2,1)S(1)} %copy-done, s32[1,1,256]{2,1,0:T(1,128)S(1)} %copy-done.1, s32[1,1]{1,0:T(1,128)S(6)} %copy.8.count_ref, f32[1,1,256]{2,1,0:T(1,128)S(1)} %copy-done.2, f32[1,1,256]{2,1,0:T(1,128)S(1)} %copy-done.3, s32[1,1]{1,0:T(1,128)S(6)} %copy.9.radius_ref), custom_call_target="tpu_custom_call" | custom-call | tf_op jit(solution)/shard_map/pallas_call | solution.py:404
  92.1 1.0 %copy.10 = bf16[1,2,2048,128]{3,2,1,0:T(8,128)(2,1)} copy(bf16[1,2,2048,128]{3,2,1,0:T(8,128)(2,1)S(1)} %shard_map.64) | data formatting | bytes 2097152
Async XLA Ops:
  0.0 1.4 %copy-start.2 = (f32[1,1,256]{2,1,0:T(1,128)S(1)}, f32[1,1,256]{2,1,0:T(1,128)}, u32[]{:S(2)}) copy-start(f32[1,1,256]{2,1,0:T(1,128)} %value_ref.1) | copy-start | bytes 3076
  0.0 1.4 %copy-start.3 = (f32[1,1,256]{2,1,0:T(1,128)S(1)}, f32[1,1,256]{2,1,0:T(1,128)}, u32[]{:S(2)}) copy-start(f32[1,1,256]{2,1,0:T(1,128)} %var_ref.1) | copy-start | bytes 3076
  0.7 0.7 copy-start.1
  1.4 1.2 %copy-start = (bf16[1,2,2048,128]{3,2,1,0:T(8,128)(2,1)S(1)}, bf16[1,2,2048,128]{3,2,1,0:T(8,128)(2,1)}, u32[]{:S(2)}) copy-start(bf16[1,2,2048,128]{3,2,1,0:T(8,128)(2,1)} %state_ref.1) | copy-start | bytes 3145732

commit v4 on v3

--- a/solution.py
+++ b/solution.py
@@ -251,8 +251,22 @@
     def folded(block):
         return block + pltpu.roll(block, K, 1)
 
-    uppers, lowers, scales, drive_rows = [], [], [], []
-    for a in range(2):
+    def diag_rhs(hi, lo):
+        return jnp.concatenate(
+            [
+                jnp.concatenate([hi * left_bf, hi * right_bf], axis=0),
+                jnp.concatenate([lo * left_bf, lo * right_bf], axis=0),
+            ],
+            axis=1,
+        )
+
+    def times(parts, rhs):
+        out = dot(jnp.concatenate([x for part in parts for x in part], axis=0), rhs)
+        sides = out[:, : 2 * K] + out[:, 2 * K :]
+        return [sides[2 * i * K : (2 * i + 1) * K] + sides[(2 * i + 1) * K : 2 * (i + 1) * K] for i in range(len(parts))]
+
+    def solve(a):
+        uppers, lowers, scales, drive_rows = [], [], [], []
         dx = 2 * a - 1
         side = 6 * a + 1
         rho, spread, drive, both = weighted(side, dx, 0, a)
@@ -278,68 +292,47 @@
             drive_rows.append(jnp.where(left_row, drives[r : r + 1], drives[r + 1 : r + 2]))
             uppers.append(system / scale)
 
-    def diag_rhs(hi, lo):
-        def blocks(x):
-            return jnp.concatenate([x * left_bf, x * right_bf], axis=0)
-
-        return blocks(hi), blocks(lo)
-
-    def times(hi, lo, rhs):
-        rhs_hi, rhs_lo = rhs
-        return dot(
-            jnp.concatenate([hi, lo], axis=1), jnp.concatenate([rhs_hi, rhs_hi], axis=0)
-        ) + dot(hi, rhs_lo)
-
-    next_uppers = []
-    for upper in uppers:
-        hi, lo = split(upper)
-        next_uppers.append(1.5 * upper - 0.5 * times(hi, lo, diag_rhs(hi, lo)))
-        lowers.append(1.5 * eye - 0.5 * upper)
-
-    def sweep(_, carry):
-        cur_uppers, cur_lowers = carry
-        new_uppers, new_lowers = [], []
-        for upper, lower in zip(cur_uppers, cur_lowers):
-            upper_hi, upper_lo = split(upper)
-            lower_hi, lower_lo = split(lower)
-            near = times(lower_hi, lower_lo, diag_rhs(upper_hi, upper_lo))
-            near_hi, near_lo = split(near)
-            stacked = times(
-                jnp.concatenate([upper_hi, lower_hi], axis=0),
-                jnp.concatenate([upper_lo, lower_lo], axis=0),
-                diag_rhs(near_hi, near_lo),
-            )
-            new_uppers.append(1.5 * upper - 0.5 * stacked[:K])
-            new_lowers.append(1.5 * lower - 0.5 * stacked[K:])
-        return tuple(new_uppers), tuple(new_lowers)
-
-    uppers, lowers = lax.fori_loop(1, NSI - 1, sweep, (tuple(next_uppers), tuple(lowers)))
-
-    mixings = []
-    for pair in range(NR):
-        upper, lower = uppers[pair], lowers[pair]
-        upper_hi, upper_lo = split(upper)
-        lower_hi, lower_lo = split(lower)
-        near = times(lower_hi, lower_lo, diag_rhs(upper_hi, upper_lo))
-        lower = 1.5 * lower - 0.5 * times(lower_hi, lower_lo, diag_rhs(*split(near)))
-        inv_root = lower / jnp.sqrt(scales[pair])
-        half = halves_sum_exact(inv_root * drive_rows[pair])
-        shift = jnp.sum(half * inv_root, axis=0, keepdims=True)
-        transform = (K - 1.0) ** 0.5 * inv_root + shift
-        mean = halves_sum_exact(transform) * (1.0 / K)
-        mixings.append((1.0 / K + transform - mean).astype(bf16))
-    for a in range(2):
-        for half in range(2):
-            first = 4 * a + 2 * half
-            mix_ref[a, half] = jnp.concatenate(mixings[first : first + 2], axis=1)
-
-    each_peer(lambda target, source: entry_copy(target, source).wait())
-
-    def band(a, _):
-        mix_lo = mix_ref[a, 0]
-        mix_hi = mix_ref[a, 1]
-
-        first_col = pl.multiple_of(a * BLK, BLK)
+        next_uppers = []
+        for upper in uppers:
+            halves = split(upper)
+            next_uppers.append(1.5 * upper - 0.5 * times([halves], diag_rhs(*halves))[0])
+            lowers.append(1.5 * eye - 0.5 * upper)
+
+        def sweep(_, carry):
+            cur_uppers, cur_lowers = carry
+            upper_halves = [split(upper) for upper in cur_uppers]
+            lower_halves = [split(lower) for lower in cur_lowers]
+            nears = [times([lo], diag_rhs(*up))[0] for lo, up in zip(lower_halves, upper_halves)]
+            steps = [
+                times([up, lo], diag_rhs(*split(near)))
+                for up, lo, near in zip(upper_halves, lower_halves, nears)
+            ]
+            new_uppers = [1.5 * upper - 0.5 * step[0] for upper, step in zip(cur_uppers, steps)]
+            new_lowers = [1.5 * lower - 0.5 * step[1] for lower, step in zip(cur_lowers, steps)]
+            return tuple(new_uppers), tuple(new_lowers)
+
+        uppers, lowers = lax.fori_loop(1, NSI - 1, sweep, (tuple(next_uppers), tuple(lowers)))
+
+        lower_halves = [split(lower) for lower in lowers]
+        nears = [times([lo], diag_rhs(*split(upper)))[0] for lo, upper in zip(lower_halves, uppers)]
+        steps = [times([lo], diag_rhs(*split(near)))[0] for lo, near in zip(lower_halves, nears)]
+        mixings = []
+        for pair in range(NR // 2):
+            lower = 1.5 * lowers[pair] - 0.5 * steps[pair]
+            inv_root = lower / jnp.sqrt(scales[pair])
+            half = halves_sum_exact(inv_root * drive_rows[pair])
+            shift = jnp.sum(half * inv_root, axis=0, keepdims=True)
+            transform = (K - 1.0) ** 0.5 * inv_root + shift
+            mean = halves_sum_exact(transform) * (1.0 / K)
+            mixings.append((1.0 / K + transform - mean).astype(bf16))
+        mix_ref[0] = jnp.concatenate(mixings[:2], axis=1)
+        mix_ref[1] = jnp.concatenate(mixings[2:], axis=1)
+
+    def move(a):
+        mix_lo = mix_ref[0]
+        mix_hi = mix_ref[1]
+
+        first_col = a * BLK
         for group in range(K // 16):
             members = pl.ds(group * 16, 16)
             cells = jnp.concatenate(
@@ -370,11 +363,10 @@
 
         each_peer(lambda target, _source: exit_copy(a, target, me).start())
         own_exit(a).start()
-        return 0
 
     def exit_copy(a, target, owner):
         return pltpu.make_async_remote_copy(
-            src_ref=mixed_ref.at[target, :, pl.ds(pl.multiple_of(a * BLK, BLK), BLK), :],
+            src_ref=mixed_ref.at[target, :, pl.ds(a * BLK, BLK), :],
             dst_ref=out_ref.at[
                 0, :, pl.ds(pl.multiple_of(owner * COLS + a * BLK, BLK), BLK), :
             ],
@@ -386,12 +378,16 @@
 
     def own_exit(a):
         return pltpu.make_async_copy(
-            mixed_ref.at[me, :, pl.ds(pl.multiple_of(a * BLK, BLK), BLK), :],
+            mixed_ref.at[me, :, pl.ds(a * BLK, BLK), :],
             out_ref.at[0, :, pl.ds(pl.multiple_of(me * COLS + a * BLK, BLK), BLK), :],
             own_sem.at[1 + a],
         )
 
-    lax.fori_loop(0, 2, band, 0)
+    for a in range(2):
+        solve(a)
+        if a == 0:
+            each_peer(lambda target, source: entry_copy(target, source).wait())
+        move(a)
 
     for a in range(2):
         own_exit(a).wait()
@@ -417,7 +413,7 @@
             pltpu.VMEM((BLK, K, LEV * ROWS), bf16),
             pltpu.VMEM((BLK, K, LEV * ROWS), bf16),
             pltpu.VMEM((2, GRAM_ROWS, 2 * K), f32),
-            pltpu.VMEM((2, 2, K, 4 * K), bf16),
+            pltpu.VMEM((2, K, 4 * K), bf16),
             dma((3,)),
             dma((N_MEM,)),
             dma((N_MEM,)),

time: 94.2 us -> 83.7 us (0.89)
  Pallas kernels: 89.5 us -> 79.6 us
    pallas_call x1, Pallas kernels: 89.5 us -> 79.6 us  [local(): pl.pallas_call(kernel, out_shape=jax.ShapeDtypeStruct(state.shape, bf16),...]
where the time goes in v4:
time: 83.7 us; the launch traced here: 83.2 us
  Pallas kernels  79.6 us (95%)
  local copies, waits for them, and re-layouts  2.2 us (3%)
  between operations  1.39 us (2%)
    pallas_call x1, Pallas kernels, local(): pl.pallas_call(kernel, out_shape=jax.ShapeDtypeStruct(state.shape, bf16),...  79.6 us
    unnamed x9, local copies, waits for them, and re-layouts  2.2 us

profile of v4, /device:TPU:1, one launch (start us, length us, event | category | flops | bytes accessed | tf_op | source)
XLA Modules:
  0.0 83.2 jit_solution(4620083509042870363)
XLA Ops:
  0.0 0.0 copy-start.2
  0.0 0.0 copy-start.3
  0.7 0.0 copy-start.1
  1.4 0.0 copy-done.2
  1.4 0.0 copy-done.3
  1.4 0.0 copy-done.1
  1.4 0.0 copy-start
  1.4 1.2 %copy-done = bf16[1,2,2048,128]{3,2,1,0:T(8,128)(2,1)S(1)} copy-done((bf16[1,2,2048,128]{3,2,1,0:T(8,128)(2,1)S(1)}, bf16[1,2,2048,128]{3,2,1,0:T(8,128)(2,1)}, u32[]{:S(2)}) %copy-start) | copy-done | bytes 1048600
  2.6 79.6 %shard_map.64 = bf16[1,2,2048,128]{3,2,1,0:T(8,128)(2,1)S(1)} custom-call(bf16[1,2,2048,128]{3,2,1,0:T(8,128)(2,1)S(1)} %copy-done, s32[1,1,256]{2,1,0:T(1,128)S(1)} %copy-done.1, s32[1,1]{1,0:T(1,128)S(6)} %copy.8.count_ref, f32[1,1,256]{2,1,0:T(1,128)S(1)} %copy-done.2, f32[1,1,256]{2,1,0:T(1,128)S(1)} %copy-done.3, s32[1,1]{1,0:T(1,128)S(6)} %copy.9.radius_ref), custom_call_target="tpu_custom_call" | custom-call | tf_op jit(solution)/shard_map/pallas_call | solution.py:400
  82.2 1.0 %copy.10 = bf16[1,2,2048,128]{3,2,1,0:T(8,128)(2,1)} copy(bf16[1,2,2048,128]{3,2,1,0:T(8,128)(2,1)S(1)} %shard_map.64) | data formatting | bytes 2097152
Async XLA Ops:
  0.0 1.4 %copy-start.2 = (f32[1,1,256]{2,1,0:T(1,128)S(1)}, f32[1,1,256]{2,1,0:T(1,128)}, u32[]{:S(2)}) copy-start(f32[1,1,256]{2,1,0:T(1,128)} %value_ref.1) | copy-start | bytes 3076
  0.0 1.4 %copy-start.3 = (f32[1,1,256]{2,1,0:T(1,128)S(1)}, f32[1,1,256]{2,1,0:T(1,128)}, u32[]{:S(2)}) copy-start(f32[1,1,256]{2,1,0:T(1,128)} %var_ref.1) | copy-start | bytes 3076
  0.7 0.7 copy-start.1
  1.4 1.2 %copy-start = (bf16[1,2,2048,128]{3,2,1,0:T(8,128)(2,1)S(1)}, bf16[1,2,2048,128]{3,2,1,0:T(8,128)(2,1)}, u32[]{:S(2)}) copy-start(bf16[1,2,2048,128]{3,2,1,0:T(8,128)(2,1)} %state_ref.1) | copy-start | bytes 3145732

commit v5 on v4

--- a/solution.py
+++ b/solution.py
@@ -19,6 +19,7 @@
 NR = ROWS // BLK
 OWN = 4
 BULK = (3, 5, 8)
+VMEM_GRANT = 67043328 - 2300 * 1024
 GRAM_ROWS = NR * K + 16
 
 MESH = pl.DeviceIdType.MESH
@@ -70,14 +71,29 @@
 
 
 def kernel(
-    state_ref, index_ref, count_ref, value_ref, var_ref, radius_ref, out_ref,
+    state_hbm, index_hbm, count_ref, value_hbm, var_hbm, radius_ref, out_ref,
+    state_ref, index_ref, value_ref, var_ref,
     index_all, seen_ref, raw_ref,
     tile_ref, mixed_ref, ens_ref, halo_ref, z_ref, o_ref, gram_ref, mix_ref,
-    own_sem, index_send, index_recv, seen_send, seen_recv, in_send, in_recv, meta_send, meta_recv, ens_send, ens_recv, out_send, out_recv,
+    arg_sem, own_sem, index_send, index_recv, seen_send, seen_recv, in_send, in_recv, meta_send, meta_recv, ens_send, ens_recv, out_send, out_recv,
 ):
     me = lax.axis_index("mem")
     gy = lax.axis_index("gy")
     barrier = pltpu.get_barrier_semaphore()
+
+    arguments = [
+        pltpu.make_async_copy(src, dst, arg_sem.at[i])
+        for i, (src, dst) in enumerate(
+            (
+                (index_hbm, index_ref),
+                (value_hbm, value_ref),
+                (var_hbm, var_ref),
+                (state_hbm, state_ref),
+            )
+        )
+    ]
+    for copy in arguments:
+        copy.start()
 
     each_peer = peers_of(me)
 
@@ -90,8 +106,10 @@
             device = (rem(me + dx + N_MEM, N_MEM), rem(gy + dy + N_GY, N_GY))
             pl.semaphore_signal(barrier, inc=1, device_id=device, device_id_type=MESH)
 
+    for copy in arguments:
+        copy.wait()
     slots = index_ref[0]
-    live = lax.broadcasted_iota(jnp.int32, (1, OBS), 1) < count_ref[...]
+    live = lax.broadcasted_iota(jnp.int32, (1, OBS), 1) < count_ref[0, 0]
     cell = lax.div(slots, jnp.int32(ROWS))
     meta = jnp.concatenate(
         [
@@ -105,7 +123,7 @@
         axis=0,
     )
     halo_ref[OWN] = meta
-    radius = jnp.broadcast_to(radius_ref[...], (1, OBS)).astype(f32)
+    radius = jnp.full((1, OBS), radius_ref[0, 0], jnp.int32).astype(f32)
     reach_sq = radius * radius
     pl.semaphore_wait(barrier, N_MEM - 1 + 6)
 
@@ -113,8 +131,8 @@
         return pltpu.make_async_remote_copy(
             src_ref=state_ref.at[0, :, pl.ds(pl.multiple_of(target * COLS, COLS), COLS), :],
             dst_ref=tile_ref.at[slot],
-            send_sem=in_send.at[target],
-            recv_sem=in_recv.at[slot],
+            send_sem=in_send.at[0],
+            recv_sem=in_recv.at[0],
             device_id=(target, gy),
             device_id_type=MESH,
         )
@@ -136,8 +154,8 @@
         return pltpu.make_async_remote_copy(
             src_ref=index_ref.at[0],
             dst_ref=index_all.at[slot],
-            send_sem=index_send.at[target],
-            recv_sem=index_recv.at[slot],
+            send_sem=index_send.at[0],
+            recv_sem=index_recv.at[0],
             device_id=(target, gy),
             device_id_type=MESH,
         )
@@ -146,14 +164,24 @@
         return pltpu.make_async_remote_copy(
             src_ref=seen_ref.at[target],
             dst_ref=raw_ref.at[slot],
-            send_sem=seen_send.at[target],
-            recv_sem=seen_recv.at[slot],
+            send_sem=seen_send.at[0],
+            recv_sem=seen_recv.at[0],
             device_id=(target, gy),
             device_id_type=MESH,
         )
 
     def start_entry(target, _source):
         entry_copy(target, me).start()
+
+    def finish_all(ref, send, recv):
+        pltpu.make_async_remote_copy(
+            src_ref=ref,
+            dst_ref=ref,
+            send_sem=send,
+            recv_sem=recv,
+            device_id=(rem(me + 1, N_MEM), gy),
+            device_id_type=MESH,
+        ).wait()
 
     each_peer(lambda target, _source: index_copy(target, me).start())
     meta_copies = [side_copy(halo_ref.at[OWN], halo_ref, meta_send, meta_recv, i) for i in range(8)]
@@ -168,7 +196,7 @@
     own_in.start()
     own_in.wait()
     index_all[me] = index_ref[0]
-    each_peer(lambda target, source: index_copy(target, source).wait())
+    finish_all(index_all.at[pl.ds(0, N_MEM - 1)], index_send.at[0], index_recv.at[0])
 
     row_iota = lax.broadcasted_iota(jnp.int32, (ROWS, OBS), 0)
     cell_iota = lax.broadcasted_iota(jnp.int32, (LEV * COLS, OBS), 0)
@@ -186,7 +214,7 @@
     raw_ref[me] = seen_ref[me]
     each_peer(lambda target, _source: seen_copy(target, me).start())
     each_peer(start_entry, *BULK[:2])
-    each_peer(lambda target, source: seen_copy(target, source).wait())
+    finish_all(raw_ref.at[pl.ds(0, N_MEM - 1)], seen_send.at[0], seen_recv.at[0])
 
     ens_ref[OWN] = raw_ref[:, 0, :].astype(bf16)
     ens_copies = [side_copy(ens_ref.at[OWN], ens_ref, ens_send, ens_recv, i) for i in range(8)]
@@ -370,8 +398,8 @@
             dst_ref=out_ref.at[
                 0, :, pl.ds(pl.multiple_of(owner * COLS + a * BLK, BLK), BLK), :
             ],
-            send_sem=out_send.at[a, target],
-            recv_sem=out_recv.at[a, owner],
+            send_sem=out_send.at[a],
+            recv_sem=out_recv.at[a],
             device_id=(target, gy),
             device_id_type=MESH,
         )
@@ -386,23 +414,35 @@
     for a in range(2):
         solve(a)
         if a == 0:
-            each_peer(lambda target, source: entry_copy(target, source).wait())
+            finish_all(tile_ref.at[pl.ds(0, N_MEM - 1)], in_send.at[0], in_recv.at[0])
         move(a)
 
     for a in range(2):
         own_exit(a).wait()
 
-        each_peer(lambda target, source: exit_copy(a, target, source).wait())
+        band_cells = mixed_ref.at[pl.ds(0, N_MEM - 1), :, pl.ds(a * BLK, BLK), :]
+        finish_all(band_cells, out_send.at[a], out_recv.at[a])
 
 
 def local(state, obs_index, obs_count, obs_value, obs_var, radius):
     dma = pltpu.SemaphoreType.DMA
     return pl.pallas_call(
         kernel,
-        out_shape=jax.ShapeDtypeStruct(state.shape, bf16),
-        in_specs=[pl.BlockSpec(memory_space=pltpu.VMEM)] * 6,
+        out_shape=pltpu.VMEM(state.shape, bf16),
+        in_specs=[
+            pl.BlockSpec(memory_space=pl.ANY),
+            pl.BlockSpec(memory_space=pl.ANY),
+            pl.BlockSpec(memory_space=pltpu.SMEM),
+            pl.BlockSpec(memory_space=pl.ANY),
+            pl.BlockSpec(memory_space=pl.ANY),
+            pl.BlockSpec(memory_space=pltpu.SMEM),
+        ],
         out_specs=pl.BlockSpec(memory_space=pl.ANY),
         scratch_shapes=[
+            pltpu.VMEM(state.shape, bf16),
+            pltpu.VMEM((1, 1, OBS), jnp.int32),
+            pltpu.VMEM((1, 1, OBS), f32),
+            pltpu.VMEM((1, 1, OBS), f32),
             pltpu.VMEM((N_MEM, 1, OBS), jnp.int32),
             pltpu.VMEM((N_MEM, 1, OBS), f32),
             pltpu.VMEM((N_MEM, 1, OBS), f32),
@@ -414,22 +454,23 @@
             pltpu.VMEM((BLK, K, LEV * ROWS), bf16),
             pltpu.VMEM((2, GRAM_ROWS, 2 * K), f32),
             pltpu.VMEM((2, K, 4 * K), bf16),
+            dma((4,)),
             dma((3,)),
-            dma((N_MEM,)),
-            dma((N_MEM,)),
-            dma((N_MEM,)),
-            dma((N_MEM,)),
-            dma((N_MEM,)),
-            dma((N_MEM,)),
+            dma((1,)),
+            dma((1,)),
+            dma((1,)),
+            dma((1,)),
+            dma((1,)),
+            dma((1,)),
             dma((8,)),
             dma((8,)),
             dma((8,)),
             dma((8,)),
-            dma((2, N_MEM)),
-            dma((2, N_MEM)),
+            dma((2,)),
+            dma((2,)),
         ],
         compiler_params=pltpu.CompilerParams(
-            collective_id=0, has_side_effects=True, vmem_limit_bytes=24 * 2**20
+            collective_id=0, has_side_effects=True, vmem_limit_bytes=VMEM_GRANT
         ),
     )(state, obs_index, obs_count, obs_value, obs_var, radius)
 

time: 83.7 us -> 75.9 us (0.907)
  Pallas kernels: 79.6 us -> 73.5 us
  local copies, waits for them, and re-layouts: 2.2 us -> 0.97 us
    pallas_call x1, Pallas kernels: 79.6 us -> 73.5 us  [local(): pl.pallas_call(kernel, out_shape=pltpu.VMEM(state.shape, bf16), in_specs=...]
    unnamed x9 -> x1, local copies, waits for them, and re-layouts: 2.2 us -> 0.97 us
where the time goes in v5:
time: 75.9 us; the launch traced here: 75.8 us
  Pallas kernels  73.5 us (97%)
  between operations  1.3 us (2%)
  local copies, waits for them, and re-layouts  0.97 us (1%)
    pallas_call x1, Pallas kernels, local(): pl.pallas_call(kernel, out_shape=pltpu.VMEM(state.shape, bf16), in_specs=...  73.5 us

profile of v5, /device:TPU:1, one launch (start us, length us, event | category | flops | bytes accessed | tf_op | source)
XLA Modules:
  0.0 75.8 jit_solution(8642741395482860987)
XLA Ops:
  1.3 73.5 %shard_map.64 = bf16[1,2,2048,128]{3,2,1,0:T(8,128)(2,1)S(1)} custom-call(bf16[1,2,2048,128]{3,2,1,0:T(8,128)(2,1)} %state_hbm.1, s32[1,1,256]{2,1,0:T(1,128)} %index_hbm.1, s32[1,1]{1,0:T(1,128)S(6)} %copy.9.count_ref, f32[1,1,256]{2,1,0:T(1,128)} %value_hbm.1, f32[1,1,256]{2,1,0:T(1,128)} %var_hbm.1, s32[1,1]{1,0:T(1,128)S(6)} %copy.10.radius_ref), custom_call_target="tpu_custom_call" | custom-call | tf_op jit(solution)/shard_map/pallas_call | solution.py:429
  74.8 1.0 %copy.8 = bf16[1,2,2048,128]{3,2,1,0:T(8,128)(2,1)} copy(bf16[1,2,2048,128]{3,2,1,0:T(8,128)(2,1)S(1)} %shard_map.64) | data formatting | bytes 2097152

commit v6 on v5

--- a/solution.py
+++ b/solution.py
@@ -18,7 +18,7 @@
 N_GY = 8
 NR = ROWS // BLK
 OWN = 4
-BULK = (3, 5, 8)
+BULK = (4, 6, 8)
 VMEM_GRANT = 67043328 - 2300 * 1024
 GRAM_ROWS = NR * K + 16
 

time: 75.9 us -> 76.9 us (1.013)
  Pallas kernels: 73.5 us -> 74.4 us
    pallas_call x1, Pallas kernels: 73.5 us -> 74.4 us  [local(): pl.pallas_call(kernel, out_shape=pltpu.VMEM(state.shape, bf16), in_specs=...]
where the time goes in v6:
time: 76.9 us; the launch traced here: 76.7 us
  Pallas kernels  74.4 us (97%)
  between operations  1.3 us (2%)
  local copies, waits for them, and re-layouts  0.97 us (1%)
    pallas_call x1, Pallas kernels, local(): pl.pallas_call(kernel, out_shape=pltpu.VMEM(state.shape, bf16), in_specs=...  74.4 us

profile of v6, /device:TPU:1, one launch (start us, length us, event | category | flops | bytes accessed | tf_op | source)
XLA Modules:
  0.0 76.7 jit_solution(17152913046891315928)
XLA Ops:
  1.3 74.4 %shard_map.64 = bf16[1,2,2048,128]{3,2,1,0:T(8,128)(2,1)S(1)} custom-call(bf16[1,2,2048,128]{3,2,1,0:T(8,128)(2,1)} %state_hbm.1, s32[1,1,256]{2,1,0:T(1,128)} %index_hbm.1, s32[1,1]{1,0:T(1,128)S(6)} %copy.9.count_ref, f32[1,1,256]{2,1,0:T(1,128)} %value_hbm.1, f32[1,1,256]{2,1,0:T(1,128)} %var_hbm.1, s32[1,1]{1,0:T(1,128)S(6)} %copy.10.radius_ref), custom_call_target="tpu_custom_call" | custom-call | tf_op jit(solution)/shard_map/pallas_call | solution.py:429
  75.7 1.0 %copy.8 = bf16[1,2,2048,128]{3,2,1,0:T(8,128)(2,1)} copy(bf16[1,2,2048,128]{3,2,1,0:T(8,128)(2,1)S(1)} %shard_map.64) | data formatting | bytes 2097152
